TPU v7x, 128 devices: a whole 4x4x4 slice. The times are simulated.
128 devices in a mesh: dp: 8 (over x, core), tensor: 16 (over z, y).
Axes of the slice: x: 4, y: 4, z: 4, core: 2. Of those that a mesh axis runs over, the one named last changes fastest.
Arguments:
- tokens: bfloat16 [192, 8, 4096], P('dp'), may hold values from -6 to 6
- norm_gain: float32 [4096], replicated, may hold values from 0.1 to 1.9
- in_weight: bfloat16 [4096, 2, 8192], P(None, None, 'tensor'), may hold values from -0.09375 to 0.09375
- group_weight: bfloat16 [4096, 2048], P(None, 'tensor'), may hold values from -0.09375 to 0.09375
- step_weight: bfloat16 [4096, 128], P(None, 'tensor'), may hold values from -0.09375 to 0.09375
- value_kernel: bfloat16 [4, 8192], P(None, 'tensor'), may hold values from -3 to 3
- value_offset: bfloat16 [8192], P('tensor'), may hold values from -3 to 3
- group_kernel: bfloat16 [4, 2048], P(None, 'tensor'), may hold values from -3 to 3
- group_offset: bfloat16 [2048], P('tensor'), may hold values from -3 to 3
- step_bias: float32 [128], P('tensor'), may hold values from -4 to 1
- decay_rate: float32 [128], P('tensor'), may hold values from 0.05 to 2
- skip_gain: float32 [128], P('tensor'), may hold values from 0.5 to 2
- out_gain: float32 [8192], P('tensor'), may hold values from 0.1 to 1.9
- out_weight: bfloat16 [8192, 4096], P('tensor'), may hold values from -0.0625 to 0.0625
- scan_state: bfloat16 [192, 128, 64, 128], P('dp', 'tensor'), may hold values from -6 to 6
- value_cache: bfloat16 [192, 3, 8192], P('dp', None, 'tensor'), may hold values from -6 to 6
- group_cache: bfloat16 [192, 3, 2048], P('dp', None, 'tensor'), may hold values from -6 to 6
- accepted: int32 [192], P('dp'), may hold values from 0 to 8, as said below
- draft_lengths: int32 [192], P('dp'), may hold values from 1 to 8, as said below
- live_flags: int32 [192], P('dp'), may hold values 0 or 1
Outputs:
- layer_out: bfloat16 [192, 8, 4096], P('dp')
- kept_state: bfloat16 [192, 128, 64, 128], P('dp', 'tensor')
- value_kept: bfloat16 [192, 3, 8192], P('dp', None, 'tensor')
- group_kept: bfloat16 [192, 3, 2048], P('dp', None, 'tensor')
- accepted_total: int32 [1], replicated
Inputs may be any that keep to these rules, and one draw needn't show every extreme that they name: `draft_lengths`: positions at or after a request's draft length are padding. `accepted`: never more than the same request's draft length.
All inputs are finite; a program needn't handle non-finite values.
Results may differ from a plain program's by a relative error of at most 0.012.
Values may be sent and summed in bfloat16 or wider, within the bound.
A program may use at most 128 MiB of HBM per device.

v0:
```python
import functools

import jax
import jax.numpy as jnp
from jax import lax
from jax.sharding import Mesh
from jax.sharding import PartitionSpec as P

DP = ("dp_0", "dp_1")


EPSILON = 1e-05


def over_axes(shard, axes):
    return functools.reduce(lax.psum, axes, shard)


def swapped(value, axis, distance):
    mask = 2**distance
    pairs = [(source, source ^ mask) for source in range(lax.axis_size(axis))]
    return lax.ppermute(value, axis, pairs)


def split_up(shard, dim, devices):
    before, after = (shard.shape[:dim], shard.shape[dim + 1 :])
    return jnp.moveaxis(shard.reshape(*before, devices, -1, *after), dim, 0)


def sum_at_owner(shard, axis, dim):
    devices = lax.axis_size(axis)
    pieces = lax.all_to_all(split_up(shard, dim, devices), axis, 0, 0, tiled=True)
    return jnp.sum(pieces.astype(jnp.float32), axis=0)


def joined_along(pieces, dim):
    lengths = list(pieces.shape[1:])
    lengths[dim] *= pieces.shape[0]
    return jnp.moveaxis(pieces, 0, dim).reshape(lengths)


def copy_for_each(shard, axis):
    devices = lax.axis_size(axis)
    return lax.all_to_all(
        jnp.broadcast_to(shard[None], (devices, *shard.shape)), axis, 0, 0, tiled=True
    )


def gather_directly(shard, axis, dim):
    return joined_along(copy_for_each(shard, axis), dim)


def convolve(window, fresh_rows, kernel, offset):
    sequence = jnp.concatenate([window, fresh_rows], axis=1)
    length = fresh_rows.shape[1]
    summed = jnp.zeros(fresh_rows.shape, jnp.float32) + offset.astype(jnp.float32)
    for tap_index in range(kernel.shape[0]):
        summed = summed + kernel[tap_index].astype(jnp.float32) * sequence[
            :, tap_index : tap_index + length
        ].astype(jnp.float32)
    return (jax.nn.silu(summed), sequence)


def keep_window(sequence, kept_count, width_rows):
    return jax.vmap(
        lambda single, start_row: lax.dynamic_slice_in_dim(single, start_row, width_rows, 0)
    )(sequence, kept_count)


def local(
    tokens,
    norm_gain,
    in_weight,
    group_weight,
    step_weight,
    value_kernel,
    value_offset,
    group_kernel,
    group_offset,
    step_bias,
    decay_rate,
    skip_gain,
    out_gain,
    out_weight,
    scan_state,
    value_cache,
    group_cache,
    accepted,
    draft_lengths,
    live_flags,
):
    requests, positions, model_width = tokens.shape
    row_total = requests * positions
    head_count = step_bias.shape[0]
    inner_dev = value_offset.shape[0]
    head_dim = inner_dev // head_count
    tap_count = value_kernel.shape[0]
    kept_count = accepted * live_flags
    accepted_total = over_axes(jnp.sum(kept_count), DP).reshape(1)
    flat_rows = tokens.reshape(row_total, model_width).astype(jnp.float32)
    normed = (
        flat_rows
        * lax.rsqrt(jnp.mean(flat_rows * flat_rows, axis=1, keepdims=True) + EPSILON)
        * norm_gain
    ).astype(jnp.bfloat16)
    parity = lax.axis_index("tensor") % 2
    in_flat = in_weight.reshape(in_weight.shape[0], 2 * inner_dev)
    inner_sum = jnp.dot(normed, in_flat, preferred_element_type=jnp.float32)
    group_sum = jnp.dot(normed, group_weight, preferred_element_type=jnp.float32)
    step_raw = jnp.dot(normed, step_weight, preferred_element_type=jnp.float32)
    inner_proj = inner_sum.astype(jnp.bfloat16).reshape(requests, positions, 2 * inner_dev)
    gate_part = inner_proj[:, :, :inner_dev]
    value_part = inner_proj[:, :, inner_dev:]
    group_proj = group_sum.astype(jnp.bfloat16).reshape(requests, positions, group_weight.shape[1])
    value_conv, value_seq = convolve(value_cache, value_part, value_kernel, value_offset)
    own_conv, group_seq = convolve(group_cache, group_proj, group_kernel, group_offset)
    other_conv = swapped(own_conv, "tensor", 0)
    input_map = jnp.where(parity == 0, own_conv, other_conv)
    output_map = jnp.where(parity == 0, other_conv, own_conv)
    values = value_conv.reshape(requests, positions, head_count, head_dim)
    step_size = jax.nn.softplus(step_raw.reshape(requests, positions, head_count) + step_bias)
    log_decay = -step_size * decay_rate
    prefix = jnp.concatenate(
        [jnp.zeros((requests, 1, head_count), jnp.float32), jnp.cumsum(log_decay, axis=1)], axis=1
    )
    after_step = prefix[:, 1:]
    alignment = jnp.einsum("rsn,rjn->rsj", output_map, input_map)
    causal = (jnp.arange(positions)[:, None] >= jnp.arange(positions)[None, :])[None, :, :, None]
    spread = after_step[:, :, None, :] - after_step[:, None, :, :]
    weights_mix = (
        jnp.where(causal, jnp.exp(jnp.where(causal, spread, 0.0)), 0.0)
        * step_size[:, None, :, :]
        * alignment[:, :, :, None]
    )
    within = jnp.einsum("rsjh,rjhp->rshp", weights_mix, values)
    initial = scan_state.astype(jnp.float32)
    carried = jnp.einsum("rhpn,rsn->rshp", initial, output_map) * jnp.exp(after_step)[:, :, :, None]
    head_out = within + carried + skip_gain[:, None] * values
    one_hot = (jnp.arange(positions + 1)[None, :] == kept_count[:, None]).astype(jnp.float32)
    prefix_kept = jnp.sum(one_hot[:, :, None] * prefix, axis=1)
    before_kept = (jnp.arange(positions)[None, :] < kept_count[:, None])[:, :, None]
    keep_weight = (
        jnp.where(
            before_kept,
            jnp.exp(jnp.where(before_kept, prefix_kept[:, None, :] - after_step, 0.0)),
            0.0,
        )
        * step_size
    )
    weighted = keep_weight[:, :, :, None] * values
    kept_state = (
        jnp.exp(prefix_kept)[:, :, None, None] * initial
        + jnp.einsum("rjhp,rjn->rhpn", weighted, input_map)
    ).astype(jnp.bfloat16)
    gated = head_out.reshape(row_total, inner_dev) * jax.nn.silu(
        gate_part.reshape(row_total, inner_dev).astype(jnp.float32)
    )
    own_squares = jnp.sum(gated * gated, axis=1)
    other_squares = swapped(own_squares, "tensor", 0)
    scale_rows = lax.rsqrt((own_squares + other_squares) / (2 * inner_dev) + EPSILON)
    valid_rows = (jnp.arange(positions)[None, :] < draft_lengths[:, None]) & (
        live_flags[:, None] == 1
    )
    normalized = jnp.where(
        valid_rows.reshape(row_total, 1), gated * scale_rows[:, None] * out_gain, 0.0
    ).astype(jnp.bfloat16)
    own_rows = sum_at_owner(
        jnp.dot(normalized, out_weight, preferred_element_type=jnp.float32).astype(jnp.bfloat16),
        "tensor",
        0,
    ).astype(jnp.bfloat16)
    layer_rows = gather_directly(own_rows, "tensor", 0)
    value_kept = keep_window(value_seq, kept_count, tap_count - 1)
    group_kept = keep_window(group_seq, kept_count, tap_count - 1)
    return (
        layer_rows.reshape(requests, positions, model_width),
        kept_state,
        value_kept,
        group_kept,
        accepted_total,
    )


def solution(mesh):
    torus = Mesh(mesh.devices.reshape(4, 2, mesh.shape["tensor"]), ("dp_0", "dp_1", "tensor"))
    in_specs = (
        P(DP, None, None),
        P(),
        P(None, None, "tensor"),
        P(None, "tensor"),
        P(None, "tensor"),
        P(None, "tensor"),
        P("tensor"),
        P(None, "tensor"),
        P("tensor"),
        P("tensor"),
        P("tensor"),
        P("tensor"),
        P("tensor"),
        P("tensor", None),
        P(DP, "tensor", None, None),
        P(DP, None, "tensor"),
        P(DP, None, "tensor"),
        P(DP),
        P(DP),
        P(DP),
    )
    out_specs = (
        P(DP, None, None),
        P(DP, "tensor", None, None),
        P(DP, None, "tensor"),
        P(DP, None, "tensor"),
        P(),
    )
    return jax.shard_map(local, mesh=torus, in_specs=in_specs, out_specs=out_specs, check_vma=False)
```

profile of v0, /device:TPU:0, one launch (start us, length us, event | category | flops | bytes accessed | tf_op | source)
XLA Modules:
  0.0 123.6 jit_solution(17323254633286002984)
XLA Ops:
  0.7 1.9 %fusion = f32[24,8]{1,0:T(8,128)S(1)} fusion(bf16[24,8,4096]{2,1,0:T(8,128)(2,1)} %param.20), kind=kLoop, calls=%fused_computation.7 | loop fusion | flops 2359104 | bytes 1573632 | tf_op jit(solution)/shard_map/reduce_sum | solution.py:103
  4.9 2.1 %fusion.29 = bf16[24,8,128]{2,1,0:T(8,128)(2,1)S(1)} fusion(bf16[4096,128]{1,0:T(8,128)(2,1)S(1)} %copy-done, bf16[24,8,4096]{2,1,0:T(8,128)(2,1)} %param.20, f32[4096]{0:T(1024)} %param.21, f32[192]{0:T(256)S(1)} %rsqrt.16), kind=kOutput, calls=%fused_computation.27 | convolution fusion | flops 204496896 | bytes 2687744 | tf_op jit(solution)/shard_map/dot_general | solution.py:109
  7.0 1.8 %collective-permute-start = (bf16[24,8,128]{2,0,1:T(8,128)(2,1)S(1)}, bf16[24,8,128]{2,0,1:T(8,128)(2,1)}, u32[]{:S(2)}, u32[]{:S(2)}) collective-permute-start(bf16[24,8,128]{2,0,1:T(8,128)(2,1)S(1)} %divide_multiply_fusion.1), channel_id=1, source_target_pairs={{0,1},{1,0},{2,3},{3,2},{4,5},{5,4},{6,7},{7,6},{8,9},{9,8},{10,11... | collective-permute-start | bytes 147464 | tf_op jit(solution)/shard_map/ppermute | solution.py:22
  10.7 9.4 %copy.54 = bf16[512,8,2,512]{3,1,2,0:T(8,128)(2,1)} copy(bf16[512,8,2,512]{3,2,1,0:T(2,128)(2,1)} %bitcast.96) | data formatting | bytes 16777216
  20.2 5.3 %fusion.17 = bf16[24,8,1024]{2,1,0:T(8,128)(2,1)S(1)} fusion(bf16[4096,1024]{1,0:T(8,128)(2,1)} %bitcast.97, bf16[24,8,4096]{2,1,0:T(8,128)(2,1)S(1)} %copy-done.2, f32[4096]{0:T(1024)S(1)} %copy-done.17, f32[24,8]{1,0:T(8,128)S(1)} %add_rsqrt_fusion), kind=kOutput, calls=%fused_computation.23 | convolution fusion | flops 1613955072 | bytes 10371840 | tf_op jit(solution)/shard_map/dot_general | solution.py:108
  30.6 1.2 reshape.254
  34.0 1.5 %convolution_bitcast_fusion = f32[24,8,8,64]{3,1,2,0:T(8,128)S(1)} fusion(f32[24,8,8,64]{3,2,1,0:T(8,128)S(1)} %reshape.239, f32[24,8,8]{2,1,0:T(8,128)S(1)} %fusion.61, f32[24,8,8]{1,2,0:T(8,128)} %copy.39, f32[24,8,8]{1,2,0:T(8,128)} %copy.37, pred[8,8]{1,0:T(8,128)(4,1)S(1)} %iota_compare_fusion.3), kind=kOutput, calls=%fused_computation.18 | convolution fusion | flops 1634304 | bytes 804928 | tf_op jit(solution)/shard_map/rsjh,rjhp->rshp/dot_general | solution.py:135
  35.6 5.4 %multiply_reduce_fusion = (f32[24,8]{1,0:T(8,128)S(1)}, f32[24,8,8,64]{3,1,2,0:T(8,128)}) fusion(f32[24,8,8,64]{3,2,1,0:T(8,128)S(1)} %reshape.254, f32[24,8,8,64]{3,2,1,0:T(8,128)S(1)} %reshape.239, f32[8]{0:T(128)S(1)} %copy-done.21, f32[24,8,8,64]{3,1,2,0:T(8,128)S(1)} %convolution_bitcast_fusion, f32[24,8,8]{1,2,0:T(8,128)} %copy.44, ...), kind=kOutput, calls=%fused_computation.29 | convolution fusion | flops 26246976 | bytes 4774688 | tf_op jit(solution)/shard_map/rhpn,rsn->rshp/dot_general | solution.py:137
  41.8 1.3 %copy.46 = f32[24,8,8,64]{3,2,1,0:T(8,128)S(1)} copy(f32[24,8,8,64]{3,1,2,0:T(8,128)} %get-tuple-element.24) | data formatting | bytes 786432 | tf_op jit(solution)/shard_map/add | solution.py:138
  43.3 1.6 %collective-permute-done.1 = f32[192]{0:T(256)S(1)} collective-permute-done((f32[192]{0:T(256)S(1)}, f32[192]{0:T(256)S(1)}, u32[]{:S(2)}, u32[]{:S(2)}) %collective-permute-start.1) | collective-permute-done | bytes 800 | tf_op jit(solution)/shard_map/ppermute | solution.py:22
  44.9 4.4 %convolution_convert_fusion = bf16[192,4096]{1,0:T(8,128)(2,1)} fusion(bf16[512,4096]{1,0:T(8,128)(2,1)} %param.33, f32[192,512]{1,0:T(8,128)S(1)} %reshape.241, f32[512]{0:T(512)S(1)} %copy-done.18, f32[192]{0:T(256)S(1)} %add_rsqrt_fusion.1, pred[192]{0:T(512)(128)(4,1)S(1)} %and.23, bf16[24,8,1024]{2,1,0:T(8,128)(2,1)S(1)} %copy-done.4), kind=kOutput, calls=%fused_computation.3 | convolution fusion | flops 807075840 | bytes 6360576 | tf_op jit(solution)/shard_map/dot_general | solution.py:168
  49.3 2.3 %reshape.242 = bf16[16,12,4096]{2,1,0:T(8,128)(2,1)S(1)} reshape(bf16[192,4096]{1,0:T(8,128)(2,1)} %convolution_convert_fusion) | data formatting | bytes 3145728 | tf_op jit(solution)/shard_map/reshape | solution.py:27
  51.6 35.6 %all_to_all.10 = bf16[16,12,4096]{2,1,0:T(8,128)(2,1)} all-to-all(bf16[16,12,4096]{2,1,0:T(8,128)(2,1)S(1)} %reshape.242), channel_id=1, replica_groups=mesh['dp_0'=4,'dp_1'=2,'tensor'=16] {'tensor'}, dimensions={0} | all-to-all | bytes 3145728 | tf_op jit(solution)/shard_map/all_to_all | solution.py:32
  87.3 2.0 %reduce_sum.53 = bf16[12,4096]{1,0:T(8,128)(2,1)S(1)} reduce(bf16[16,12,4096]{2,1,0:T(8,128)(2,1)} %all_to_all.10, bf16[]{:T(256)} %constant.47.clone.1), dimensions={0}, to_apply=%region_3.0 | reduce | flops 737280 | bytes 1671170 | tf_op jit(solution)/shard_map/reduce_sum | solution.py:33
  89.2 1.6 %broadcast_in_dim.48 = bf16[16,12,4096]{2,1,0:T(8,128)(2,1)} broadcast(bf16[12,4096]{1,0:T(8,128)(2,1)S(1)} %reduce_sum.53), dimensions={1,2} | broadcast | bytes 1671168 | tf_op jit(solution)/shard_map/broadcast_in_dim | solution.py:45
  90.8 3.7 %all-to-all-start.1 = ((bf16[16,12,4096]{2,1,0:T(8,128)(2,1)}), bf16[16,12,4096]{2,1,0:T(8,128)(2,1)S(1)}, u32[]{:S(2)}, u32[]{:S(2)}) async-start(bf16[16,12,4096]{2,1,0:T(8,128)(2,1)} %broadcast_in_dim.48), calls=%async_computation.1 | async-start | bytes 4194304 | tf_op jit(solution)/shard_map/all_to_all | solution.py:44
  94.5 9.5 %psum.14 = s32[]{:T(128)} all-reduce(s32[]{:T(128)} %get-tuple-element.5), channel_id=1, replica_groups=mesh['dp_0'=4,'dp_1'=2,'tensor'=16] {'dp_0'}, use_global_device_ids=true, to_apply=%region_6.7 | all-reduce | flops 1 | bytes 8 | tf_op jit(solution)/shard_map/psum | solution.py:16
  104.1 2.4 %psum.15 = s32[1]{0:T(128)} all-reduce(s32[1]{0:T(128)} %bitcast.21), channel_id=1, replica_groups=mesh['dp_0'=4,'dp_1'=2,'tensor'=16] {'dp_1'}, use_global_device_ids=true, to_apply=%region_7.8 | all-reduce | flops 1 | bytes 8 | tf_op jit(solution)/shard_map/psum | solution.py:16
  107.1 1.6 %gather_fusion = bf16[24,3,512]{2,0,1:T(8,128)(2,1)} fusion(bf16[24,11,512]{2,0,1:T(8,128)(2,1)S(1)} %copy_dynamic-update-slice_fusion, s32[24]{0:T(128)S(1)} %fusion.73), kind=kCustom, calls=%fused_computation | custom fusion | bytes 147744 | tf_op jit(solution)/shard_map/vmap()/gather | solution.py:66
  108.8 1.4 %gather_fusion.1 = bf16[24,3,128]{2,0,1:T(8,128)(2,1)} fusion(bf16[24,11,128]{2,0,1:T(8,128)(2,1)S(1)} %copy_dynamic-update-slice_fusion.1, s32[24]{0:T(128)S(1)} %fusion.73), kind=kCustom, calls=%fused_computation.1 | custom fusion | bytes 37152 | tf_op jit(solution)/shard_map/vmap()/gather | solution.py:66
  110.2 1.4 %broadcast_multiply_fusion = bf16[24,8,8,64]{3,2,1,0:T(8,128)(2,1)S(1)} fusion(f32[24,8,8,64]{3,2,1,0:T(8,128)} %copy-done.1, f32[24,8,8]{2,1,0:T(8,128)} %get-tuple-element.9), kind=kLoop, calls=%fused_computation.45 | loop fusion | flops 196608 | bytes 595968 | tf_op jit(solution)/shard_map/mul | solution.py:150
  111.6 5.3 %add_convert_fusion = bf16[24,8,64,128]{3,2,1,0:T(8,128)(2,1)} fusion(bf16[24,8,64,128]{3,2,1,0:T(8,128)(2,1)} %param.34, f32[24,8]{1,0:T(8,128)} %exp.46, bf16[24,8,8,64]{3,2,1,0:T(8,128)(2,1)S(1)} %broadcast_multiply_fusion, bf16[24,8,128]{2,0,1:T(8,128)(2,1)S(1)} %get-tuple-element.12), kind=kOutput, calls=%fused_computation.2 | convolution fusion | flops 31457280 | bytes 6537984 | tf_op jit(solution)/shard_map/rjhp,rjn->rhpn/dot_general | solution.py:153
  116.9 5.3 %all-to-all-done.1 = bf16[16,12,4096]{2,1,0:T(8,128)(2,1)S(1)} async-done(((bf16[16,12,4096]{2,1,0:T(8,128)(2,1)}), bf16[16,12,4096]{2,1,0:T(8,128)(2,1)S(1)}, u32[]{:S(2)}, u32[]{:S(2)}) %all-to-all-start.1) | async-done | bytes 1572896 | tf_op jit(solution)/shard_map/all_to_all | solution.py:44
  122.2 1.3 %reshape_reshape.3 = bf16[24,8,4096]{2,1,0:T(8,128)(2,1)} reshape(bf16[16,12,4096]{2,1,0:T(8,128)(2,1)S(1)} %all-to-all-done.1) | data formatting | bytes 3145728 | tf_op jit(solution)/shard_map/reshape;reshape | solution.py:176
  (82 shorter events, 13.2 us)
Async XLA Ops:
  0.6 4.2 %copy-start = (bf16[4096,128]{1,0:T(8,128)(2,1)S(1)}, bf16[4096,128]{1,0:T(8,128)(2,1)}, u32[]{:S(2)}) copy-start(bf16[4096,128]{1,0:T(8,128)(2,1)} %param.23) | copy-start | bytes 3145732
  0.6 8.2 %copy-start.12 = (s32[24]{0:T(128)S(1)}, s32[24]{0:T(128)}, u32[]{:S(2)}) copy-start(s32[24]{0:T(128)} %param.37) | copy-start | bytes 292
  0.7 8.2 %copy-start.13 = (s32[24]{0:T(128)S(1)}, s32[24]{0:T(128)}, u32[]{:S(2)}) copy-start(s32[24]{0:T(128)} %param.39) | copy-start | bytes 292
  7.0 13.1 %copy-start.5 = (bf16[24,8,128]{2,0,1:T(8,128)(2,1)}, bf16[24,8,128]{2,0,1:T(8,128)(2,1)S(1)}, u32[]{:S(2)}) copy-start(bf16[24,8,128]{2,0,1:T(8,128)(2,1)S(1)} %divide_multiply_fusion.1) | copy-start | bytes 147460
  7.0 26.0 %collective-permute-start = (bf16[24,8,128]{2,0,1:T(8,128)(2,1)S(1)}, bf16[24,8,128]{2,0,1:T(8,128)(2,1)}, u32[]{:S(2)}, u32[]{:S(2)}) collective-permute-start(bf16[24,8,128]{2,0,1:T(8,128)(2,1)S(1)} %divide_multiply_fusion.1), channel_id=1, source_target_pairs={{0,1},{1,0},{2,3},{3,2},{4,5},{5,4},{6,7},{7,6},{8,9},{9,8},{10,11... | collective-permute-start | bytes 147464 | tf_op jit(solution)/shard_map/ppermute | solution.py:22
  9.5 10.7 %copy-start.9 = (s32[24]{0:T(128)}, s32[24]{0:T(128)S(1)}, u32[]{:S(2)}) copy-start(s32[24]{0:T(128)S(1)} %get-tuple-element.6) | copy-start | bytes 292
  10.7 9.4 %copy-start.2 = (bf16[24,8,4096]{2,1,0:T(8,128)(2,1)S(1)}, bf16[24,8,4096]{2,1,0:T(8,128)(2,1)}, u32[]{:S(2)}) copy-start(bf16[24,8,4096]{2,1,0:T(8,128)(2,1)} %param.20) | copy-start | bytes 4718596
  10.7 9.4 %copy-start.17 = (f32[4096]{0:T(1024)S(1)}, f32[4096]{0:T(1024)}, u32[]{:S(2)}) copy-start(f32[4096]{0:T(1024)} %param.21) | copy-start | bytes 49156
  20.2 6.9 %copy-start.6 = (bf16[24,3,512]{2,0,1:T(8,128)(2,1)S(1)}, bf16[24,3,512]{2,0,1:T(8,128)(2,1)}, u32[]{:S(2)}) copy-start(bf16[24,3,512]{2,0,1:T(8,128)(2,1)} %param.35) | copy-start | bytes 221188
  20.2 6.9 %copy-start.8 = (bf16[4,512]{1,0:T(4,128)(2,1)S(1)}, bf16[4,512]{1,0:T(4,128)(2,1)}, u32[]{:S(2)}) copy-start(bf16[4,512]{1,0:T(4,128)(2,1)} %param.25) | copy-start | bytes 12292
  20.2 6.9 %copy-start.11 = (bf16[512]{0:T(512)(128)(2,1)S(1)}, bf16[512]{0:T(512)(128)(2,1)}, u32[]{:S(2)}) copy-start(bf16[512]{0:T(512)(128)(2,1)} %param.26) | copy-start | bytes 3076
  20.2 7.0 %copy-start.16 = (bf16[4096,8]{0,1:T(8,128)(2,1)S(1)}, bf16[4096,8]{0,1:T(8,128)(2,1)}, u32[]{:S(2)}) copy-start(bf16[4096,8]{0,1:T(8,128)(2,1)} %param.24) | copy-start | bytes 196612
  20.2 7.0 %copy-start.19 = (f32[8]{0:T(128)S(1)}, f32[8]{0:T(128)}, u32[]{:S(2)}) copy-start(f32[8]{0:T(128)} %param.30) | copy-start | bytes 100
  20.2 7.0 %copy-start.20 = (f32[8]{0:T(128)S(1)}, f32[8]{0:T(128)}, u32[]{:S(2)}) copy-start(f32[8]{0:T(128)} %param.29) | copy-start | bytes 100
  27.1 0.9 copy-start.7
  29.9 5.7 %copy-start.21 = (f32[8]{0:T(128)S(1)}, f32[8]{0:T(128)}, u32[]{:S(2)}) copy-start(f32[8]{0:T(128)} %param.31) | copy-start | bytes 100
  32.2 8.8 %copy-start.1 = (f32[24,8,8,64]{3,2,1,0:T(8,128)}, f32[24,8,8,64]{3,2,1,0:T(8,128)S(1)}, u32[]{:S(2)}) copy-start(f32[24,8,8,64]{3,2,1,0:T(8,128)S(1)} %reshape.239) | copy-start | bytes 1179652
  35.5 6.1 %copy-start.14 = (s32[24]{0:T(128)S(1)}, s32[24]{0:T(128)}, u32[]{:S(2)}) copy-start(s32[24]{0:T(128)} %param.38) | copy-start | bytes 292
  35.5 6.1 %copy-start.15 = (pred[24]{0:T(512)(128)(4,1)S(1)}, pred[24]{0:T(512)(128)(4,1)}, u32[]{:S(2)}) copy-start(pred[24]{0:T(512)(128)(4,1)} %broadcast_compare_fusion) | copy-start | bytes 76
  35.5 9.3 %copy-start.4 = (bf16[24,8,1024]{2,1,0:T(8,128)(2,1)S(1)}, bf16[24,8,1024]{2,1,0:T(8,128)(2,1)}, u32[]{:S(2)}) copy-start(bf16[24,8,1024]{2,1,0:T(8,128)(2,1)} %copy-done.3) | copy-start | bytes 1179652
  35.5 9.3 %copy-start.18 = (f32[512]{0:T(512)S(1)}, f32[512]{0:T(512)}, u32[]{:S(2)}) copy-start(f32[512]{0:T(512)} %param.32) | copy-start | bytes 6148
  41.0 3.8 %collective-permute-start.1 = (f32[192]{0:T(256)S(1)}, f32[192]{0:T(256)S(1)}, u32[]{:S(2)}, u32[]{:S(2)}) collective-permute-start(f32[192]{0:T(256)S(1)} %reduce_sum.52), channel_id=1, source_target_pairs={{0,1},{1,0},{2,3},{3,2},{4,5},{5,4},{6,7},{7,6},{8,9},{9,8},{10,11... | collective-permute-start | bytes 2312 | tf_op jit(solution)/shard_map/ppermute | solution.py:22
  89.2 17.9 %copy-start.10 = (s32[24]{0:T(128)S(1)}, s32[24]{0:T(128)}, u32[]{:S(2)}) copy-start(s32[24]{0:T(128)} %copy-done.9) | copy-start | bytes 292
  90.8 31.4 %all-to-all-start.1 = ((bf16[16,12,4096]{2,1,0:T(8,128)(2,1)}), bf16[16,12,4096]{2,1,0:T(8,128)(2,1)S(1)}, u32[]{:S(2)}, u32[]{:S(2)}) async-start(bf16[16,12,4096]{2,1,0:T(8,128)(2,1)} %broadcast_in_dim.48), calls=%async_computation.1 | async-start | bytes 4194304 | tf_op jit(solution)/shard_map/all_to_all | solution.py:44
  (1 other events, 0.7 us)
where the time goes:
time: 124 us
  blocking collectives  47.6 us (38%)
  local copies, waits for them, and re-layouts  25.6 us (21%)
  matrix products  24.7 us (20%)
  other arithmetic  11.6 us (9%)
  waiting for transfers between devices  6.89 us (6%)
  starting transfers between devices  6.08 us (5%)
    all_to_all x1, blocking collectives, sum_at_owner(): lax.all_to_all(split_up(shard, dim, devices), axis, 0, 0, tiled=True)  35.6 us
    psum x2, blocking collectives, over_axes(): return functools.reduce(lax.psum, axes, shard)  12 us
    unnamed x47, local copies, waits for them, and re-layouts  11 us
    dot_general x1, matrix products, local(): jnp.einsum('rhpn,rsn->rshp', initial, output_map)  5.38 us
    all_to_all x1, waiting for transfers between devices, copy_for_each(): lax.all_to_all(jnp.broadcast_to(shard[None], (devices, *shard.shape)), ax...  5.34 us
    dot_general x1, matrix products, local(): jnp.einsum('rjhp,rjn->rhpn', weighted, input_map)  5.29 us
    dot_general x1, matrix products, local(): inner_sum = jnp.dot(normed, in_flat, preferred_element_type=jnp.float32)  5.29 us
    dot_general x1, matrix products, local(): jnp.dot(normalized, out_weight, preferred_element_type=jnp.float32)  4.4 us
  transfers between devices with their start and end apart: 3, of which 2 were waited for; matrix products, arithmetic and copies ran while one was open for 28% of the time, Pallas kernels for 0%

commit v1 on v0

--- a/solution.py
+++ b/solution.py
@@ -1,19 +1,14 @@
-import functools
-
 import jax
 import jax.numpy as jnp
 from jax import lax
-from jax.sharding import Mesh
+from jax.experimental import pallas as pl
+from jax.experimental.pallas import tpu as pltpu
 from jax.sharding import PartitionSpec as P
 
-DP = ("dp_0", "dp_1")
+DP = "dp"
 
 
 EPSILON = 1e-05
-
-
-def over_axes(shard, axes):
-    return functools.reduce(lax.psum, axes, shard)
 
 
 def swapped(value, axis, distance):
@@ -22,32 +17,267 @@
     return lax.ppermute(value, axis, pairs)
 
 
-def split_up(shard, dim, devices):
-    before, after = (shard.shape[:dim], shard.shape[dim + 1 :])
-    return jnp.moveaxis(shard.reshape(*before, devices, -1, *after), dim, 0)
-
-
-def sum_at_owner(shard, axis, dim):
-    devices = lax.axis_size(axis)
-    pieces = lax.all_to_all(split_up(shard, dim, devices), axis, 0, 0, tiled=True)
-    return jnp.sum(pieces.astype(jnp.float32), axis=0)
-
-
-def joined_along(pieces, dim):
-    lengths = list(pieces.shape[1:])
-    lengths[dim] *= pieces.shape[0]
-    return jnp.moveaxis(pieces, 0, dim).reshape(lengths)
-
-
-def copy_for_each(shard, axis):
-    devices = lax.axis_size(axis)
-    return lax.all_to_all(
-        jnp.broadcast_to(shard[None], (devices, *shard.shape)), axis, 0, 0, tiled=True
-    )
-
-
-def gather_directly(shard, axis, dim):
-    return joined_along(copy_for_each(shard, axis), dim)
+MESH = pl.DeviceIdType.MESH
+TOP, BOTTOM = pl.ds(0, 48), pl.ds(48, 48)
+
+
+def ring_places():
+    tensor = lax.axis_index("tensor")
+    z, y = tensor // 4, tensor % 4
+    along_y = [{"tensor": z * 4 + (y + d) % 4} for d in range(4)]
+    along_z = [{"tensor": ((z + d) % 4) * 4 + y} for d in range(4)]
+    return (z, y, along_z, along_y)
+
+
+def remote(src, dst, sems, place):
+    send, recv, index = sems
+    return pltpu.make_async_remote_copy(
+        src_ref=src,
+        dst_ref=dst,
+        send_sem=send.at[index],
+        recv_sem=recv.at[index],
+        device_id=place,
+        device_id_type=MESH,
+    )
+
+
+def widened_sum(*refs):
+    total = refs[0][...].astype(jnp.float32)
+    for ref in refs[1:]:
+        total = total + ref[...].astype(jnp.float32)
+    return total.astype(jnp.bfloat16)
+
+
+def exchange_kernel(
+    rows_ref,
+    weight_ref,
+    counts_ref,
+    out_ref,
+    total_ref,
+    partial,
+    first_recv,
+    first_mix,
+    first_sum,
+    second_recv,
+    second_mix,
+    count_buf,
+    send_sems,
+    recv_sems,
+    count_send,
+    count_recv,
+):
+    z, y, along_z, along_y = ring_places()
+    dp = lax.axis_index("dp")
+    barrier = pltpu.get_barrier_semaphore()
+    dp_peers = [{"dp": (dp + d) % 8} for d in range(1, 8)]
+    ring_peers = [along_z[1], along_z[3], along_y[1], along_y[3]]
+    for place in ring_peers + dp_peers:
+        pl.semaphore_signal(barrier, inc=1, device_id=place, device_id_type=MESH)
+    kept = jnp.sum(counts_ref[...].astype(jnp.float32), axis=1, keepdims=True)
+    count_buf[0] = jnp.broadcast_to(kept, (8, 128))
+    firsts = [along_y, along_z]
+    seconds = [along_z, along_y]
+    first_at = [y, z]
+    second_at = [z, y]
+    copies = []
+
+    def launch(src, dst, stage, route, slot, place):
+        copy = remote(src, dst, (send_sems, recv_sems, (stage, route, slot)), place)
+        copy.start()
+        copies.append(copy)
+        return copy
+
+    def project(route, step):
+        base = ((first_at[route] + step) % 4) * 1024
+
+        def one(j, carry):
+            columns = pl.ds(pl.multiple_of(base + j * 256, 256), 256)
+            partial[route, step, :, pl.ds(pl.multiple_of(j * 256, 256), 256)] = jnp.dot(
+                rows_ref[pl.ds(route * 96, 96), :],
+                weight_ref[:, columns],
+                preferred_element_type=jnp.float32,
+            ).astype(jnp.bfloat16)
+            return carry
+
+        lax.fori_loop(0, 4, one, 0)
+
+    project(0, 2)
+    pl.semaphore_wait(barrier, 11)
+    count_copies = []
+    for d in range(1, 8):
+        copy = remote(count_buf.at[0], count_buf.at[d], (count_send, count_recv, d), dp_peers[d - 1])
+        copy.start()
+        count_copies.append(copy)
+
+    def first_step(route):
+        unit = partial.at[route]
+        plus, minus = (firsts[route][1], firsts[route][3])
+        a = launch(unit.at[2, TOP], first_recv.at[route, 0], 0, route, 0, plus)
+        b = launch(unit.at[2, BOTTOM], first_recv.at[route, 1], 0, route, 1, minus)
+        return [a, b]
+
+    held = [first_step(0)]
+    project(1, 2)
+    held.append(first_step(1))
+    for route in range(2):
+        project(route, 1)
+        held[route].append(
+            launch(
+                partial.at[route, 1, BOTTOM], first_recv.at[route, 3], 0, route, 3, firsts[route][1]
+            )
+        )
+    for route in range(2):
+        project(route, 3)
+        held[route].append(
+            launch(
+                partial.at[route, 3, TOP], first_recv.at[route, 4], 0, route, 4, firsts[route][3]
+            )
+        )
+    for route in range(2):
+        held[route][0].wait_recv()
+        first_mix[route, 0] = widened_sum(first_recv.at[route, 0], partial.at[route, 1, TOP])
+        held[route].append(
+            launch(first_mix.at[route, 0], first_recv.at[route, 2], 0, route, 2, firsts[route][1])
+        )
+        held[route][1].wait_recv()
+        first_mix[route, 1] = widened_sum(first_recv.at[route, 1], partial.at[route, 3, BOTTOM])
+        held[route].append(
+            launch(first_mix.at[route, 1], first_recv.at[route, 5], 0, route, 5, firsts[route][3])
+        )
+    for route in range(2):
+        project(route, 0)
+    for half in range(2):
+        for route in range(2):
+            rows = (TOP, BOTTOM)[half]
+            waits = ((3, 4), (2, 5))[half]
+            for index in waits:
+                held[route][index].wait_recv()
+            plus_ref = first_recv.at[route, 2 + half]
+            minus_ref = first_recv.at[route, 4 + half]
+            for j in range(4):
+                columns = pl.ds(j * 256, 256)
+                first_sum[route, j, rows] = widened_sum(
+                    partial.at[route, 0, rows, columns],
+                    plus_ref.at[:, columns],
+                    minus_ref.at[:, columns],
+                )
+    late = []
+    for route in range(2):
+        at = second_at[route]
+        plus, minus = (seconds[route][1], seconds[route][3])
+        unit = [first_sum.at[route, (at + k) % 4] for k in range(4)]
+        landing = second_recv.at[route]
+        late.append(
+            [
+                launch(unit[2].at[TOP], landing.at[0], 1, route, 0, plus),
+                launch(unit[2].at[BOTTOM], landing.at[1], 1, route, 1, minus),
+                launch(unit[1].at[BOTTOM], landing.at[3], 1, route, 3, plus),
+                launch(unit[3].at[TOP], landing.at[4], 1, route, 4, minus),
+            ]
+        )
+    for route in range(2):
+        at = second_at[route]
+        plus, minus = (seconds[route][1], seconds[route][3])
+        landing = second_recv.at[route]
+        late[route][0].wait_recv()
+        second_mix[route, 0] = widened_sum(landing.at[0], first_sum.at[route, (at + 1) % 4, TOP])
+        late[route].append(
+            launch(second_mix.at[route, 0], landing.at[2], 1, route, 2, plus)
+        )
+        late[route][1].wait_recv()
+        second_mix[route, 1] = widened_sum(landing.at[1], first_sum.at[route, (at + 3) % 4, BOTTOM])
+        late[route].append(
+            launch(second_mix.at[route, 1], landing.at[5], 1, route, 5, minus)
+        )
+
+    def spot(route, half, first, second, width):
+        column = pl.multiple_of(first * 1024 + second * 256, 256)
+        return out_ref.at[pl.ds(route * 96 + half * 48, 48), pl.ds(column, width)]
+
+    for half in range(2):
+        for route in range(2):
+            rows = (TOP, BOTTOM)[half]
+            waits = ((3, 4), (2, 5))[half]
+            for index in waits:
+                late[route][index].wait_recv()
+            own = spot(route, half, first_at[route], second_at[route], 256)
+            own[...] = widened_sum(
+                first_sum.at[route, second_at[route], rows],
+                second_recv.at[route, 2 + half],
+                second_recv.at[route, 4 + half],
+            )
+
+    def spread(stage, places, piece):
+        started = []
+        for route in range(2):
+            plus, minus = (places[route][1], places[route][3])
+            started.append(
+                [
+                    launch(piece(route, 0, 0), piece(route, 0, 0), stage, route, 0, plus),
+                    launch(piece(route, 1, 0), piece(route, 1, 0), stage, route, 1, minus),
+                    launch(piece(route, 1, 0), piece(route, 1, 0), stage, route, 2, plus),
+                    launch(piece(route, 0, 0), piece(route, 0, 0), stage, route, 3, minus),
+                ]
+            )
+        for route in range(2):
+            plus, minus = (places[route][1], places[route][3])
+            started[route][0].wait_recv()
+            started[route].append(
+                launch(piece(route, 0, 3), piece(route, 0, 3), stage, route, 4, plus)
+            )
+            started[route][1].wait_recv()
+            started[route].append(
+                launch(piece(route, 1, 1), piece(route, 1, 1), stage, route, 5, minus)
+            )
+        for route in range(2):
+            for index in range(2, 6):
+                started[route][index].wait_recv()
+
+    def near(route, half, k):
+        return spot(route, half, first_at[route], (second_at[route] + k) % 4, 256)
+
+    def far(route, half, k):
+        return spot(route, half, (first_at[route] + k) % 4, 0, 1024)
+
+    spread(2, seconds, near)
+    spread(3, firsts, far)
+    for copy in count_copies:
+        copy.wait_recv()
+    everyone = count_buf[0]
+    for d in range(1, 8):
+        everyone = everyone + count_buf[d]
+    total_ref[...] = everyone.astype(jnp.int32)
+    for copy in copies + count_copies:
+        copy.wait_send()
+
+
+def exchange(rows, weight, counts):
+    half = pltpu.VMEM((2, 6, 48, 1024), jnp.bfloat16)
+    return pl.pallas_call(
+        exchange_kernel,
+        out_shape=(
+            jax.ShapeDtypeStruct((192, 4096), jnp.bfloat16),
+            jax.ShapeDtypeStruct((8, 128), jnp.int32),
+        ),
+        in_specs=[pl.BlockSpec(memory_space=pltpu.VMEM)] * 3,
+        out_specs=(pl.BlockSpec(memory_space=pltpu.VMEM),) * 2,
+        scratch_shapes=[
+            pltpu.VMEM((2, 4, 96, 1024), jnp.bfloat16),
+            half,
+            pltpu.VMEM((2, 2, 48, 1024), jnp.bfloat16),
+            pltpu.VMEM((2, 4, 96, 256), jnp.bfloat16),
+            pltpu.VMEM((2, 6, 48, 256), jnp.bfloat16),
+            pltpu.VMEM((2, 2, 48, 256), jnp.bfloat16),
+            pltpu.VMEM((8, 8, 128), jnp.float32),
+            pltpu.SemaphoreType.DMA((4, 2, 6)),
+            pltpu.SemaphoreType.DMA((4, 2, 6)),
+            pltpu.SemaphoreType.DMA((8,)),
+            pltpu.SemaphoreType.DMA((8,)),
+        ],
+        compiler_params=pltpu.CompilerParams(
+            collective_id=0, has_side_effects=True, vmem_limit_bytes=40 * 1024 * 1024
+        ),
+    )(rows, weight, counts)
 
 
 def convolve(window, fresh_rows, kernel, offset):
@@ -96,7 +326,6 @@
     head_dim = inner_dev // head_count
     tap_count = value_kernel.shape[0]
     kept_count = accepted * live_flags
-    accepted_total = over_axes(jnp.sum(kept_count), DP).reshape(1)
     flat_rows = tokens.reshape(row_total, model_width).astype(jnp.float32)
     normed = (
         flat_rows
@@ -164,12 +393,8 @@
     normalized = jnp.where(
         valid_rows.reshape(row_total, 1), gated * scale_rows[:, None] * out_gain, 0.0
     ).astype(jnp.bfloat16)
-    own_rows = sum_at_owner(
-        jnp.dot(normalized, out_weight, preferred_element_type=jnp.float32).astype(jnp.bfloat16),
-        "tensor",
-        0,
-    ).astype(jnp.bfloat16)
-    layer_rows = gather_directly(own_rows, "tensor", 0)
+    layer_rows, totals = exchange(normalized, out_weight, kept_count.reshape(1, requests))
+    accepted_total = totals[0, :1]
     value_kept = keep_window(value_seq, kept_count, tap_count - 1)
     group_kept = keep_window(group_seq, kept_count, tap_count - 1)
     return (
@@ -182,7 +407,6 @@
 
 
 def solution(mesh):
-    torus = Mesh(mesh.devices.reshape(4, 2, mesh.shape["tensor"]), ("dp_0", "dp_1", "tensor"))
     in_specs = (
         P(DP, None, None),
         P(),
@@ -212,4 +436,4 @@
         P(DP, None, "tensor"),
         P(),
     )
-    return jax.shard_map(local, mesh=torus, in_specs=in_specs, out_specs=out_specs, check_vma=False)
+    return jax.shard_map(local, mesh=mesh, in_specs=in_specs, out_specs=out_specs, check_vma=False)

time: 124 us -> 95.6 us (0.77)
  blocking collectives: 47.6 us -> 0 us
  Pallas kernels: 0 us -> 41 us
  waiting for transfers between devices: 6.89 us -> 0.01 us
  other arithmetic: 11.6 us -> 6.14 us
  starting transfers between devices: 6.08 us -> 2.37 us
  local copies, waits for them, and re-layouts: 25.6 us -> 22.6 us
  matrix products: 24.7 us -> 21.9 us
    pallas_call x0 -> x1, Pallas kernels: none -> 41 us  [exchange(): pl.pallas_call(exchange_kernel, out_shape=(jax.ShapeDtypeStruct((192, 409...]
    all_to_all x1 -> x0, blocking collectives: 35.6 us -> none  [sum_at_owner(): lax.all_to_all(split_up(shard, dim, devices), axis, 0, 0, tiled=True)]
    psum x2 -> x0, blocking collectives: 12 us -> none  [over_axes(): return functools.reduce(lax.psum, axes, shard)]
    all_to_all x1 -> x0, waiting for transfers between devices: 5.34 us -> none  [copy_for_each(): lax.all_to_all(jnp.broadcast_to(shard[None], (devices, *shard.shape)), ax...]
    dot_general x1 -> x0, matrix products: 4.4 us -> none  [local(): jnp.dot(normalized, out_weight, preferred_element_type=jnp.float32)]
    all_to_all x1 -> x0, starting transfers between devices: 3.72 us -> none  [copy_for_each(): lax.all_to_all(jnp.broadcast_to(shard[None], (devices, *shard.shape)), ax...]
    reduce_sum x2 -> x0, other arithmetic: 2.59 us -> none  [the longest x1 1.96 us: sum_at_owner(): return jnp.sum(pieces.astype(jnp.float32), axis=0)]
    unnamed x47 -> x38, local copies, waits for them, and re-layouts: 11 us -> 13.6 us
  transfers between devices with their start and end apart: 3 -> 2, of which waited for: 2 -> 0; matrix products, arithmetic and copies ran while one was open for 28% -> 34% of each run, Pallas kernels for 0% -> 0%
where the time goes in v1:
time: 95.6 us; the launch traced here: 95.1 us
  Pallas kernels  41 us (43%)
  local copies, waits for them, and re-layouts  22.6 us (24%)
  matrix products  21.9 us (23%)
  other arithmetic  6.14 us (6%)
  starting transfers between devices  2.37 us (2%)
  between operations  1.03 us (1%)
    pallas_call x1, Pallas kernels, exchange(): pl.pallas_call(exchange_kernel, out_shape=(jax.ShapeDtypeStruct((192, 409...  41 us
    unnamed x38, local copies, waits for them, and re-layouts  13.6 us
    dot_general x1, matrix products, local(): jnp.einsum('rhpn,rsn->rshp', initial, output_map)  5.55 us
    dot_general x1, matrix products, local(): jnp.einsum('rjhp,rjn->rhpn', weighted, input_map)  5.29 us
    dot_general x1, matrix products, local(): inner_sum = jnp.dot(normed, in_flat, preferred_element_type=jnp.float32)  5.27 us
    gather x2, local copies, waits for them, and re-layouts, keep_window(): lax.dynamic_slice_in_dim(single, start_row, width_rows, 0)  3.05 us
    ppermute x2, starting transfers between devices, swapped(): return lax.ppermute(value, axis, pairs)  2.37 us
    dot_general x1, matrix products, local(): step_raw = jnp.dot(normed, step_weight, preferred_element_type=jnp.float32)  2.07 us
  transfers between devices with their start and end apart: 2, of which 0 were waited for; matrix products, arithmetic and copies ran while one was open for 34% of the time, Pallas kernels for 0%

profile of v1, /device:TPU:0, one launch (start us, length us, event | category | flops | bytes accessed | tf_op | source)
XLA Modules:
  0.0 95.1 jit_solution(7190760315885487060)
XLA Ops:
  0.7 1.9 %fusion = f32[24,8]{1,0:T(8,128)S(1)} fusion(bf16[24,8,4096]{2,1,0:T(8,128)(2,1)} %param.20), kind=kLoop, calls=%fused_computation.6 | loop fusion | flops 2359104 | bytes 1573632 | tf_op jit(solution)/shard_map/reduce_sum | solution.py:332
  2.6 0.7 constant_dynamic-update-slice_fusion.1
  3.4 0.8 bitcast_convert_fusion.3
  4.2 0.7 convert_element_type.181
  4.9 2.1 %fusion.29 = bf16[24,8,128]{2,1,0:T(8,128)(2,1)S(1)} fusion(bf16[4096,128]{1,0:T(8,128)(2,1)S(1)} %copy-done, bf16[24,8,4096]{2,1,0:T(8,128)(2,1)} %param.20, f32[4096]{0:T(1024)} %param.21, f32[192]{0:T(256)S(1)} %rsqrt.16), kind=kOutput, calls=%fused_computation.26 | convolution fusion | flops 204496896 | bytes 2687744 | tf_op jit(solution)/shard_map/dot_general | solution.py:338
  7.0 1.8 %collective-permute-start = (bf16[24,8,128]{2,0,1:T(8,128)(2,1)S(1)}, bf16[24,8,128]{2,0,1:T(8,128)(2,1)}, u32[]{:S(2)}, u32[]{:S(2)}) collective-permute-start(bf16[24,8,128]{2,0,1:T(8,128)(2,1)S(1)} %divide_multiply_fusion.1), channel_id=1, source_target_pairs={{0,1},{1,0},{2,3},{3,2},{4,5},{5,4},{6,7},{7,6},{8,9},{9,8},{10,11... | collective-permute-start | bytes 147464 | tf_op jit(solution)/shard_map/ppermute | solution.py:17
  9.0 9.4 %copy.55 = bf16[512,8,2,512]{3,1,2,0:T(8,128)(2,1)} copy(bf16[512,8,2,512]{3,2,1,0:T(2,128)(2,1)} %bitcast.98) | data formatting | bytes 16777216
  18.5 5.3 %fusion.17 = bf16[24,8,1024]{2,1,0:T(8,128)(2,1)S(1)} fusion(bf16[4096,1024]{1,0:T(8,128)(2,1)} %bitcast.99, bf16[24,8,4096]{2,1,0:T(8,128)(2,1)S(1)} %copy-done.2, f32[4096]{0:T(1024)S(1)} %copy-done.13, f32[24,8]{1,0:T(8,128)S(1)} %add_rsqrt_fusion), kind=kOutput, calls=%fused_computation.22 | convolution fusion | flops 1613955072 | bytes 10371840 | tf_op jit(solution)/shard_map/dot_general | solution.py:337
  24.7 2.1 %negate_multiply_fusion = (f32[24,8,8]{2,1,0:T(8,128)S(1)}, f32[24,8,8]{2,1,0:T(8,128)S(1)}) fusion(f32[8]{0:T(128)S(1)} %copy-done.14, f32[8]{0:T(128)S(1)} %copy-done.15, bf16[4096,8]{0,1:T(8,128)(2,1)S(1)} %copy-done.12, bf16[24,8,4096]{2,1,0:T(8,128)(2,1)} %param.20, f32[4096]{0:T(1024)} %param.21, f32[24,8]{1,0:T(8,128)S(1)} %add_rsqrt_fusion), kind=kOutput, calls=%fused_computation.61 | convolution fusion | flops 15742464 | bytes 1667904 | tf_op jit(solution)/shard_map/dot_general | solution.py:339
  27.1 0.7 select_multiply_fusion
  28.0 1.6 %copy.40 = f32[24,8,8]{1,2,0:T(8,128)} copy(f32[24,8,8]{2,1,0:T(8,128)} %copy-done.4) | data formatting | bytes 12288 | tf_op jit(solution)/shard_map/jit(softplus)/select_n | solution.py:350
  29.7 0.7 copy.38
  30.4 1.6 %gather_fusion = bf16[24,3,512]{2,0,1:T(8,128)(2,1)} fusion(bf16[24,11,512]{2,0,1:T(8,128)(2,1)S(1)} %copy_dynamic-update-slice_fusion, s32[24]{0:T(128)S(1)} %get-tuple-element.9), kind=kCustom, calls=%fused_computation | custom fusion | bytes 147744 | tf_op jit(solution)/shard_map/vmap()/gather | solution.py:296
  32.1 1.4 %gather_fusion.1 = bf16[24,3,128]{2,0,1:T(8,128)(2,1)} fusion(bf16[24,11,128]{2,0,1:T(8,128)(2,1)S(1)} %copy_dynamic-update-slice_fusion.1, s32[24]{0:T(128)S(1)} %get-tuple-element.9), kind=kCustom, calls=%fused_computation.1 | custom fusion | bytes 37152 | tf_op jit(solution)/shard_map/vmap()/gather | solution.py:296
  33.5 1.1 %reshape.253 = f32[24,8,8,64]{3,2,1,0:T(8,128)} reshape(f32[24,8,512]{2,1,0:T(8,128)S(1)} %get-tuple-element.11) | data formatting | bytes 786432 | tf_op jit(solution)/shard_map/convert_element_type | solution.py:385
  34.5 1.0 %copy.45 = f32[24,8,8]{1,2,0:T(8,128)S(1)} copy(f32[24,8,8]{2,1,0:T(8,128)} %get-tuple-element.14) | data formatting | bytes 12288 | tf_op jit(solution)/shard_map/exp | solution.py:366
  35.6 0.8 broadcast_select_fusion.1
  36.6 1.5 %convolution_bitcast_fusion = f32[24,8,8,64]{3,1,2,0:T(8,128)S(1)} fusion(f32[24,8,8,64]{3,2,1,0:T(8,128)S(1)} %reshape.238, f32[24,8,8]{2,1,0:T(8,128)S(1)} %fusion.56, f32[24,8,8]{1,2,0:T(8,128)} %copy.40, f32[24,8,8]{1,2,0:T(8,128)} %copy.38, pred[8,8]{1,0:T(8,128)(4,1)S(1)} %iota_compare_fusion.3), kind=kOutput, calls=%fused_computation.17 | convolution fusion | flops 1634304 | bytes 804928 | tf_op jit(solution)/shard_map/rsjh,rjhp->rshp/dot_general | solution.py:364
  38.1 5.6 %multiply_reduce_fusion = (f32[24,8]{1,0:T(8,128)S(1)}, f32[24,8,8,64]{3,1,2,0:T(8,128)}) fusion(f32[24,8,8,64]{3,2,1,0:T(8,128)} %reshape.253, f32[24,8,8,64]{3,2,1,0:T(8,128)S(1)} %reshape.238, f32[8]{0:T(128)S(1)} %copy-done.16, f32[24,8,8,64]{3,1,2,0:T(8,128)S(1)} %convolution_bitcast_fusion, f32[24,8,8]{1,2,0:T(8,128)S(1)} %copy.45, ...), kind=kOutput, calls=%fused_computation.28 | convolution fusion | flops 26246976 | bytes 4774688 | tf_op jit(solution)/shard_map/rhpn,rsn->rshp/dot_general | solution.py:366
  43.7 0.6 collective-permute-start.1
  44.3 5.3 %add_convert_fusion = bf16[24,8,64,128]{3,2,1,0:T(8,128)(2,1)} fusion(bf16[24,8,64,128]{3,2,1,0:T(8,128)(2,1)} %param.34, f32[24,8]{1,0:T(8,128)S(1)} %exp.46, bf16[24,8,8,64]{3,2,1,0:T(8,128)(2,1)S(1)} %broadcast_multiply_fusion, bf16[24,8,128]{2,0,1:T(8,128)(2,1)S(1)} %get-tuple-element.16), kind=kOutput, calls=%fused_computation.2 | convolution fusion | flops 31457280 | bytes 6537984 | tf_op jit(solution)/shard_map/rjhp,rjn->rhpn/dot_general | solution.py:382
  50.2 2.2 %copy-done.1 = bf16[512,4096]{1,0:T(8,128)(2,1)S(1)} copy-done((bf16[512,4096]{1,0:T(8,128)(2,1)S(1)}, bf16[512,4096]{1,0:T(8,128)(2,1)}, u32[]{:S(2)}) %copy-start.1) | copy-done | bytes 4194328
  52.4 41.0 %shard_map.227 = (bf16[192,4096]{1,0:T(8,128)(2,1)S(1)}, s32[8,128]{1,0:T(8,128)S(1)}) custom-call(bf16[192,512]{1,0:T(8,128)(2,1)S(1)} %select_convert_fusion.rows_ref, bf16[512,4096]{1,0:T(8,128)(2,1)S(1)} %copy-done.1, s32[1,24]{1,0:T(1,128)S(1)} %bitcast.97), custom_call_target="tpu_custom_call" | custom-call | tf_op jit(solution)/shard_map/pallas_call | solution.py:256
  93.9 1.1 %copy.83 = bf16[24,8,4096]{2,1,0:T(8,128)(2,1)} copy(bf16[24,8,4096]{2,1,0:T(8,128)(2,1)S(1)} %bitcast.96) | data formatting | bytes 3145728
  (65 shorter events, 3.1 us)
Async XLA Ops:
  0.6 4.2 %copy-start = (bf16[4096,128]{1,0:T(8,128)(2,1)S(1)}, bf16[4096,128]{1,0:T(8,128)(2,1)}, u32[]{:S(2)}) copy-start(bf16[4096,128]{1,0:T(8,128)(2,1)} %param.23) | copy-start | bytes 3145732
  0.6 8.2 %copy-start.9 = (s32[24]{0:T(128)S(1)}, s32[24]{0:T(128)}, u32[]{:S(2)}) copy-start(s32[24]{0:T(128)} %param.37) | copy-start | bytes 292
  0.7 8.2 %copy-start.10 = (s32[24]{0:T(128)S(1)}, s32[24]{0:T(128)}, u32[]{:S(2)}) copy-start(s32[24]{0:T(128)} %param.39) | copy-start | bytes 292
  7.0 28.6 %collective-permute-start = (bf16[24,8,128]{2,0,1:T(8,128)(2,1)S(1)}, bf16[24,8,128]{2,0,1:T(8,128)(2,1)}, u32[]{:S(2)}, u32[]{:S(2)}) collective-permute-start(bf16[24,8,128]{2,0,1:T(8,128)(2,1)S(1)} %divide_multiply_fusion.1), channel_id=1, source_target_pairs={{0,1},{1,0},{2,3},{3,2},{4,5},{5,4},{6,7},{7,6},{8,9},{9,8},{10,11... | collective-permute-start | bytes 147464 | tf_op jit(solution)/shard_map/ppermute | solution.py:17
  9.0 9.5 %copy-start.2 = (bf16[24,8,4096]{2,1,0:T(8,128)(2,1)S(1)}, bf16[24,8,4096]{2,1,0:T(8,128)(2,1)}, u32[]{:S(2)}) copy-start(bf16[24,8,4096]{2,1,0:T(8,128)(2,1)} %param.20) | copy-start | bytes 4718596
  9.0 9.5 %copy-start.13 = (f32[4096]{0:T(1024)S(1)}, f32[4096]{0:T(1024)}, u32[]{:S(2)}) copy-start(f32[4096]{0:T(1024)} %param.21) | copy-start | bytes 49156
  18.4 5.4 %copy-start.5 = (bf16[24,3,512]{2,0,1:T(8,128)(2,1)S(1)}, bf16[24,3,512]{2,0,1:T(8,128)(2,1)}, u32[]{:S(2)}) copy-start(bf16[24,3,512]{2,0,1:T(8,128)(2,1)} %param.35) | copy-start | bytes 221188
  18.5 5.4 %copy-start.6 = (bf16[4,512]{1,0:T(4,128)(2,1)S(1)}, bf16[4,512]{1,0:T(4,128)(2,1)}, u32[]{:S(2)}) copy-start(bf16[4,512]{1,0:T(4,128)(2,1)} %param.25) | copy-start | bytes 12292
  18.5 5.4 %copy-start.8 = (bf16[512]{0:T(512)(128)(2,1)S(1)}, bf16[512]{0:T(512)(128)(2,1)}, u32[]{:S(2)}) copy-start(bf16[512]{0:T(512)(128)(2,1)} %param.26) | copy-start | bytes 3076
  23.7 0.9 copy-start.12
  23.8 0.9 copy-start.14
  23.8 0.9 copy-start.15
  24.0 3.0 %copy-start.11 = (s32[24]{0:T(128)S(1)}, s32[24]{0:T(128)}, u32[]{:S(2)}) copy-start(s32[24]{0:T(128)} %param.38) | copy-start | bytes 292
  26.7 1.0 %copy-start.4 = (f32[24,8,8]{2,1,0:T(8,128)}, f32[24,8,8]{2,1,0:T(8,128)S(1)}, u32[]{:S(2)}) copy-start(f32[24,8,8]{2,1,0:T(8,128)S(1)} %get-tuple-element.26) | copy-start | bytes 18436
  28.0 10.0 %copy-start.16 = (f32[8]{0:T(128)S(1)}, f32[8]{0:T(128)}, u32[]{:S(2)}) copy-start(f32[8]{0:T(128)} %param.31) | copy-start | bytes 100
  43.7 5.9 %copy-start.3 = (f32[24,8,8,64]{3,1,2,0:T(8,128)S(1)}, f32[24,8,8,64]{3,1,2,0:T(8,128)}, u32[]{:S(2)}) copy-start(f32[24,8,8,64]{3,1,2,0:T(8,128)} %get-tuple-element.28) | copy-start | bytes 1179652
  43.7 6.3 %copy-start.7 = (f32[512]{0:T(512)S(1)}, f32[512]{0:T(512)}, u32[]{:S(2)}) copy-start(f32[512]{0:T(512)} %param.32) | copy-start | bytes 6148
  43.7 6.3 %collective-permute-start.1 = (f32[192]{0:T(256)S(1)}, f32[192]{0:T(256)S(1)}, u32[]{:S(2)}, u32[]{:S(2)}) collective-permute-start(f32[192]{0:T(256)S(1)} %reduce_sum.31), channel_id=1, source_target_pairs={{0,1},{1,0},{2,3},{3,2},{4,5},{5,4},{6,7},{7,6},{8,9},{9,8},{10,11... | collective-permute-start | bytes 2312 | tf_op jit(solution)/shard_map/ppermute | solution.py:17
  50.2 2.2 %copy-start.1 = (bf16[512,4096]{1,0:T(8,128)(2,1)S(1)}, bf16[512,4096]{1,0:T(8,128)(2,1)}, u32[]{:S(2)}) copy-start(bf16[512,4096]{1,0:T(8,128)(2,1)} %weight_ref.1) | copy-start | bytes 12582916

commit v2 on v1

--- a/solution.py
+++ b/solution.py
@@ -48,12 +48,73 @@
     return total.astype(jnp.bfloat16)
 
 
-def exchange_kernel(
+def layer_kernel(
+    tokens_in,
+    gain_in,
+    in_weight_in,
+    group_weight_in,
+    step_weight_in,
+    value_kernel_in,
+    value_offset_in,
+    group_kernel_in,
+    group_offset_in,
+    step_bias_in,
+    decay_rate_in,
+    skip_gain_in,
+    out_gain_in,
+    out_weight_in,
+    state_in,
+    value_cache_in,
+    group_cache_in,
+    accepted_in,
+    lengths_in,
+    live_in,
+    out_ref,
+    kept_ref,
+    value_kept,
+    group_kept,
+    total_ref,
+    tokens,
+    gain,
+    in_weight,
+    group_weight,
+    step_weight,
+    value_kernel,
+    value_offset,
+    group_kernel,
+    group_offset,
+    step_bias,
+    decay_rate,
+    skip_gain,
+    out_gain,
+    out_weight,
+    state,
+    value_cache,
+    group_cache,
+    accepted,
+    lengths,
+    live,
+    normed,
+    spread_a,
+    spread_b,
+    inner,
+    group_rows,
+    step_rows,
+    maps,
+    map_rows,
+    carried,
+    small,
+    mixing,
+    decay_kept,
+    weighted,
+    turned,
+    input_rows,
+    gated_rows,
     rows_ref,
-    weight_ref,
-    counts_ref,
-    out_ref,
-    total_ref,
+    squares,
+    square_own,
+    square_other,
+    scale_rows,
     partial,
     first_recv,
     first_mix,
@@ -65,16 +126,336 @@
     recv_sems,
     count_send,
     count_recv,
+    swap_sems,
+    load_sems,
+    chunk_sems,
 ):
     z, y, along_z, along_y = ring_places()
     dp = lax.axis_index("dp")
+    parity = y % 2
+    mate = {"tensor": z * 4 + (y + 1 - 2 * parity)}
     barrier = pltpu.get_barrier_semaphore()
     dp_peers = [{"dp": (dp + d) % 8} for d in range(1, 8)]
     ring_peers = [along_z[1], along_z[3], along_y[1], along_y[3]]
     for place in ring_peers + dp_peers:
         pl.semaphore_signal(barrier, inc=1, device_id=place, device_id_type=MESH)
-    kept = jnp.sum(counts_ref[...].astype(jnp.float32), axis=1, keepdims=True)
-    count_buf[0] = jnp.broadcast_to(kept, (8, 128))
+    loads = {}
+
+    def load(name, src, dst, index):
+        loads[name] = pltpu.make_async_copy(src, dst, load_sems.at[index])
+        loads[name].start()
+
+    load("tokens", tokens_in, tokens, 0)
+    load("gain", gain_in, gain, 1)
+    load("group_weight", group_weight_in, group_weight, 3)
+    load("accepted", accepted_in, accepted, 17)
+    load("lengths", lengths_in, lengths, 18)
+    load("live", live_in, live, 19)
+    load("group_cache", group_cache_in, group_cache, 16)
+    load("group_kernel", group_kernel_in, group_kernel, 7)
+    load("group_offset", group_offset_in, group_offset, 8)
+    load("step_weight", step_weight_in, step_weight, 4)
+    load("step_bias", step_bias_in, step_bias, 9)
+    load("decay_rate", decay_rate_in, decay_rate, 10)
+    load("skip_gain", skip_gain_in, skip_gain, 11)
+    chunks = []
+    for index in range(4):
+        rows = pl.ds(index * 8192, 8192)
+        copy = pltpu.make_async_copy(in_weight_in.at[rows], in_weight.at[rows], chunk_sems.at[index])
+        copy.start()
+        chunks.append(copy)
+    load("value_cache", value_cache_in, value_cache, 15)
+    load("value_kernel", value_kernel_in, value_kernel, 5)
+    load("value_offset", value_offset_in, value_offset, 6)
+    load("out_gain", out_gain_in, out_gain, 12)
+    load("state", state_in, state, 14)
+    load("out_weight", out_weight_in, out_weight, 13)
+    def column(ref):
+        square = lax.broadcasted_iota(jnp.int32, (24, 24), 0) == lax.broadcasted_iota(
+            jnp.int32, (24, 24), 1
+        )
+        values = jnp.broadcast_to(ref[...].astype(jnp.float32), (24, 24))
+        return jnp.sum(jnp.where(square, values, 0.0), axis=1, keepdims=True)
+
+    loads["gain"].wait()
+    loads["tokens"].wait()
+
+    def normalize(block, carry):
+        rows = pl.ds(pl.multiple_of(block * 16, 16), 16)
+        total = jnp.zeros((16, 256), jnp.float32)
+        for part in range(16):
+            piece = tokens[rows, part * 256 : (part + 1) * 256].astype(jnp.float32)
+            total = total + piece * piece
+        mean = jnp.sum(total, axis=1, keepdims=True) / 4096.0
+        scale = jnp.broadcast_to(lax.rsqrt(mean + EPSILON), (16, 256))
+        for part in range(16):
+            columns = slice(part * 256, (part + 1) * 256)
+            piece = tokens[rows, columns].astype(jnp.float32)
+            normed[rows, columns] = (piece * scale * gain[:, columns]).astype(jnp.bfloat16)
+        return carry
+
+    lax.fori_loop(0, 12, normalize, 0)
+    loads["group_weight"].wait()
+    group_rows[...] = jnp.dot(
+        normed[...], group_weight[...], preferred_element_type=jnp.float32
+    )
+    for name in ("accepted", "lengths", "live", "group_cache", "group_kernel", "group_offset"):
+        loads[name].wait()
+    kept = column(accepted) * column(live)
+    alive = column(live) == 1.0
+    length_column = column(lengths)
+
+    def sequence_of(cache, rows):
+        early = [cache[t].astype(jnp.float32) for t in range(3)]
+        return early + [rounded(piece) for piece in rows]
+
+    def rounded(piece):
+        return piece.astype(jnp.bfloat16).astype(jnp.float32)
+
+    def convolved(sequence, taps, offset):
+        out = []
+        for s in range(8):
+            total = offset
+            for k in range(4):
+                total = total + taps[k] * sequence[s + k]
+            out.append(total / (1.0 + jnp.exp(-total)))
+        return out
+
+    def kept_rows(sequence, counts, t):
+        chosen = sequence[t]
+        for k in range(1, 9):
+            chosen = jnp.where(counts == float(k), sequence[k + t], chosen)
+        return chosen.astype(jnp.bfloat16)
+
+    group_taps = [group_kernel[k : k + 1, :].astype(jnp.float32) for k in range(4)]
+    group_sequence = sequence_of(
+        group_cache, [group_rows[pl.ds(s, 24, stride=8), :] for s in range(8)]
+    )
+    own_maps = convolved(
+        group_sequence, group_taps, group_offset[...].astype(jnp.float32).reshape(1, 128)
+    )
+    for s in range(8):
+        maps[parity, s] = own_maps[s]
+    pl.semaphore_wait(barrier, 11)
+    swap = pltpu.make_async_remote_copy(
+        src_ref=maps.at[parity],
+        dst_ref=maps.at[parity],
+        send_sem=swap_sems.at[0],
+        recv_sem=swap_sems.at[1],
+        device_id=mate,
+        device_id_type=MESH,
+    )
+    swap.start()
+    count_buf[0] = jnp.broadcast_to(jnp.sum(kept, axis=0, keepdims=True), (8, 128))
+    count_copies = []
+    for d in range(1, 8):
+        copy = remote(count_buf.at[0], count_buf.at[d], (count_send, count_recv, d), dp_peers[d - 1])
+        copy.start()
+        count_copies.append(copy)
+    for t in range(3):
+        group_kept[t] = kept_rows(group_sequence, kept, t)
+
+    for name in ("step_weight", "step_bias", "decay_rate", "skip_gain"):
+        loads[name].wait()
+    step_rows[:, 0:8] = lax.dot_general(
+        normed[...],
+        step_weight[...],
+        (((1,), (1,)), ((), ())),
+        preferred_element_type=jnp.float32,
+    )
+
+    inner[...] = jnp.zeros_like(inner)
+
+    def widen(start, spread):
+        spread[...] = in_weight[pl.ds(pl.multiple_of(start * 2048, 2048), 2048), :].astype(
+            jnp.float32
+        )
+
+    def multiply(start, spread):
+        left = normed[:, pl.ds(pl.multiple_of(start * 256, 256), 256)]
+        for part in range(2):
+            for j in range(0, 4, 2):
+                right = jnp.concatenate(
+                    [
+                        spread[pl.ds((j + i) * 2 + part, 256, stride=8), :].astype(jnp.bfloat16)
+                        for i in range(2)
+                    ],
+                    axis=1,
+                )
+                product = jnp.dot(left, right, preferred_element_type=jnp.float32)
+                for i in range(2):
+                    inner[part * 4 + j + i] += product[:, i * 128 : (i + 1) * 128]
+
+    def pair(index, carry):
+        widen(2 * index, spread_a)
+        multiply(2 * index, spread_a)
+        widen(2 * index + 1, spread_b)
+        multiply(2 * index + 1, spread_b)
+        return carry
+
+    for index in range(4):
+        chunks[index].wait()
+        lax.fori_loop(2 * index, 2 * index + 2, pair, 0)
+
+    steps, after = [], []
+    running = None
+    for s in range(8):
+        raw = step_rows[pl.ds(s, 24, stride=8), 0:8] + step_bias[...]
+        size = jnp.maximum(raw, 0.0) + jnp.log1p(jnp.exp(-jnp.abs(raw)))
+        change = -size * decay_rate[...]
+        running = change if running is None else running + change
+        steps.append(size)
+        after.append(running)
+    prefix_kept = jnp.zeros_like(running)
+    for s in range(8):
+        prefix_kept = jnp.where(kept == float(s + 1), after[s], prefix_kept)
+    for s in range(8):
+        small[pl.ds((36 + s) * 24, 24), 0:8] = jnp.exp(after[s])
+        small[pl.ds((44 + s) * 24, 24), 0:8] = (
+            jnp.where(kept > float(s), jnp.exp(prefix_kept - after[s]), 0.0) * steps[s]
+        )
+    head_decay = jnp.exp(prefix_kept)
+    for h in range(8):
+        decay_kept[h] = jnp.broadcast_to(head_decay[:, h : h + 1], (24, 128))
+    swap.wait_recv()
+    for s in range(8):
+        map_rows[pl.ds(s, 24, stride=8), :] = maps[1, s]
+        input_rows[pl.ds(s * 24, 24), :] = maps[0, s]
+        for j in range(s + 1):
+            match = jnp.sum(maps[1, s] * maps[0, j], axis=1, keepdims=True)
+            small[pl.ds((s * (s + 1) // 2 + j) * 24, 24), 0:8] = (
+                jnp.exp(after[s] - after[j]) * steps[j] * match
+            )
+    hot = (
+        lax.broadcasted_iota(jnp.int32, (8, 512), 1) // 64
+        == lax.broadcasted_iota(jnp.int32, (8, 512), 0)
+    ).astype(jnp.bfloat16)
+
+    def expand(index, carry):
+        rows = pl.ds(pl.multiple_of(index * 208, 16), 208)
+        mixing[rows, :] = jnp.dot(
+            small[rows, 0:8].astype(jnp.bfloat16), hot, preferred_element_type=jnp.float32
+        )
+        return carry
+
+    lax.fori_loop(0, 6, expand, 0)
+    loads["state"].wait()
+
+    def carry_over(index, carry):
+        for i in range(6):
+            request = index * 6 + i
+            rows = pl.ds(pl.multiple_of(request * 8, 8), 8)
+            product = lax.dot_general(
+                map_rows[rows, :].astype(jnp.bfloat16),
+                state[request],
+                (((1,), (1,)), ((), ())),
+                preferred_element_type=jnp.float32,
+            )
+            for block in range(4):
+                carried[block, rows, :] = product[:, block * 128 : (block + 1) * 128]
+        return carry
+
+    lax.fori_loop(0, 4, carry_over, 0)
+    for name in ("value_cache", "value_kernel", "value_offset", "out_gain"):
+        loads[name].wait()
+
+    offset_row = value_offset[...].astype(jnp.float32).reshape(1, 512)
+    for block in range(4):
+        columns = slice(block * 128, (block + 1) * 128)
+        lane = lax.broadcasted_iota(jnp.int32, (8, 128), 1)
+        skip = jnp.where(
+            lane < 64,
+            jnp.broadcast_to(skip_gain[:, 2 * block : 2 * block + 1], (8, 128)),
+            jnp.broadcast_to(skip_gain[:, 2 * block + 1 : 2 * block + 2], (8, 128)),
+        )
+        taps = [value_kernel[k : k + 1, columns].astype(jnp.float32) for k in range(4)]
+        offset = offset_row[:, columns]
+        for tile in range(3):
+            eight = pl.ds(tile * 8, 8)
+            counts = kept[tile * 8 : tile * 8 + 8]
+            sequence = [value_cache[t, eight, columns].astype(jnp.float32) for t in range(3)] + [
+                rounded(inner[4 + block, pl.ds(tile * 64 + s, 8, stride=8), :])
+                for s in range(8)
+            ]
+            for t in range(3):
+                value_kept[t, eight, columns] = kept_rows(sequence, counts, t)
+            values = convolved(sequence, taps, offset)
+            for s in range(8):
+                weighted[pl.ds(s * 24 + tile * 8, 8), columns] = (
+                    mixing[pl.ds((44 + s) * 24 + tile * 8, 8), columns] * values[s]
+                )
+                total = (
+                    mixing[pl.ds((36 + s) * 24 + tile * 8, 8), columns]
+                    * carried[block, pl.ds(tile * 64 + s, 8, stride=8), :]
+                    + skip * values[s]
+                )
+                for j in range(s + 1):
+                    q = s * (s + 1) // 2 + j
+                    total = total + mixing[pl.ds(q * 24 + tile * 8, 8), columns] * values[j]
+                gate = rounded(inner[block, pl.ds(tile * 64 + s, 8, stride=8), :])
+                gated = total * (gate / (1.0 + jnp.exp(-gate)))
+                square = gated * gated
+                if block:
+                    square = square + squares[s, eight]
+                squares[s, eight] = square
+                valid = jnp.logical_and(
+                    alive[tile * 8 : tile * 8 + 8],
+                    length_column[tile * 8 : tile * 8 + 8] > float(s),
+                )
+                gated_rows[block, pl.ds(tile * 64 + s, 8, stride=8), :] = jnp.where(
+                    valid, gated * out_gain[:, columns], 0.0
+                )
+    lanes = lax.broadcasted_iota(jnp.int32, (24, 128), 1)
+    own = jnp.zeros((24, 128), jnp.float32)
+    for s in range(8):
+        own = jnp.where(lanes == s, jnp.sum(squares[s], axis=1, keepdims=True), own)
+    square_own[...] = own
+    square_swap = pltpu.make_async_remote_copy(
+        src_ref=square_own,
+        dst_ref=square_other,
+        send_sem=swap_sems.at[2],
+        recv_sem=swap_sems.at[3],
+        device_id=mate,
+        device_id_type=MESH,
+    )
+    square_swap.start()
+    for block in range(4):
+        rows_ref[:, block * 128 : (block + 1) * 128] = gated_rows[block].astype(jnp.bfloat16)
+    loads["out_weight"].wait()
+    weight_ref = out_weight
+    turned[...] = jnp.transpose(weighted[...]).astype(jnp.bfloat16)
+    square_swap.wait_recv()
+    scales = lax.rsqrt((square_own[...] + square_other[...]) / 1024.0 + EPSILON)
+    for s in range(8):
+        scale_rows[pl.ds(s, 24, stride=8), :] = jnp.broadcast_to(scales[:, s : s + 1], (24, 128))
+
+    def keep_states():
+        owner = lax.rem(lax.broadcasted_iota(jnp.int32, (192, 128), 0), 24)
+
+        def keep(index, carry):
+            inputs = input_rows[...]
+            right = jnp.concatenate(
+                [
+                    jnp.where(owner == 2 * index + i, inputs, 0.0).astype(jnp.bfloat16)
+                    for i in range(2)
+                ],
+                axis=1,
+            )
+            for h in range(8):
+                update = jnp.dot(
+                    turned[h * 64 : (h + 1) * 64, :], right, preferred_element_type=jnp.float32
+                )
+                for i in range(2):
+                    request = 2 * index + i
+                    decay = decay_kept[h, pl.ds(request, 1), :]
+                    before = state[request, h * 64 : (h + 1) * 64, :].astype(jnp.float32)
+                    kept_ref[request, h * 64 : (h + 1) * 64, :] = (
+                        decay * before + update[:, i * 128 : (i + 1) * 128]
+                    ).astype(jnp.bfloat16)
+            return carry
+
+        lax.fori_loop(0, 12, keep, 0)
+
     firsts = [along_y, along_z]
     seconds = [along_z, along_y]
     first_at = [y, z]
@@ -92,22 +473,20 @@
 
         def one(j, carry):
             columns = pl.ds(pl.multiple_of(base + j * 256, 256), 256)
-            partial[route, step, :, pl.ds(pl.multiple_of(j * 256, 256), 256)] = jnp.dot(
+            product = jnp.dot(
                 rows_ref[pl.ds(route * 96, 96), :],
                 weight_ref[:, columns],
                 preferred_element_type=jnp.float32,
+            )
+            scale = scale_rows[pl.ds(route * 96, 96), :]
+            partial[route, step, :, pl.ds(pl.multiple_of(j * 256, 256), 256)] = (
+                product * jnp.concatenate([scale, scale], axis=1)
             ).astype(jnp.bfloat16)
             return carry
 
         lax.fori_loop(0, 4, one, 0)
 
     project(0, 2)
-    pl.semaphore_wait(barrier, 11)
-    count_copies = []
-    for d in range(1, 8):
-        copy = remote(count_buf.at[0], count_buf.at[d], (count_send, count_recv, d), dp_peers[d - 1])
-        copy.start()
-        count_copies.append(copy)
 
     def first_step(route):
         unit = partial.at[route]
@@ -146,6 +525,7 @@
         )
     for route in range(2):
         project(route, 0)
+    keep_states()
     for half in range(2):
         for route in range(2):
             rows = (TOP, BOTTOM)[half]
@@ -246,24 +626,68 @@
     everyone = count_buf[0]
     for d in range(1, 8):
         everyone = everyone + count_buf[d]
-    total_ref[...] = everyone.astype(jnp.int32)
-    for copy in copies + count_copies:
+    total_ref[0] = jnp.sum(everyone[0:1, 0:1]).astype(jnp.int32)
+    for copy in copies + count_copies + [swap, square_swap]:
         copy.wait_send()
 
 
-def exchange(rows, weight, counts):
-    half = pltpu.VMEM((2, 6, 48, 1024), jnp.bfloat16)
+def layer(*operands):
     return pl.pallas_call(
-        exchange_kernel,
+        layer_kernel,
         out_shape=(
             jax.ShapeDtypeStruct((192, 4096), jnp.bfloat16),
-            jax.ShapeDtypeStruct((8, 128), jnp.int32),
+            jax.ShapeDtypeStruct((24, 512, 128), jnp.bfloat16),
+            jax.ShapeDtypeStruct((3, 24, 512), jnp.bfloat16),
+            jax.ShapeDtypeStruct((3, 24, 128), jnp.bfloat16),
+            jax.ShapeDtypeStruct((1,), jnp.int32),
         ),
-        in_specs=[pl.BlockSpec(memory_space=pltpu.VMEM)] * 3,
-        out_specs=(pl.BlockSpec(memory_space=pltpu.VMEM),) * 2,
+        in_specs=[pl.BlockSpec(memory_space=pltpu.HBM)] * 20,
+        out_specs=(pl.BlockSpec(memory_space=pltpu.VMEM),) * 4
+        + (pl.BlockSpec(memory_space=pltpu.SMEM),),
         scratch_shapes=[
+            pltpu.VMEM((192, 4096), jnp.bfloat16),
+            pltpu.VMEM((1, 4096), jnp.float32),
+            pltpu.VMEM((32768, 128), jnp.bfloat16),
+            pltpu.VMEM((4096, 128), jnp.bfloat16),
+            pltpu.VMEM((8, 4096), jnp.bfloat16),
+            pltpu.VMEM((4, 512), jnp.bfloat16),
+            pltpu.VMEM((512,), jnp.bfloat16),
+            pltpu.VMEM((4, 128), jnp.bfloat16),
+            pltpu.VMEM((128,), jnp.bfloat16),
+            pltpu.VMEM((1, 8), jnp.float32),
+            pltpu.VMEM((1, 8), jnp.float32),
+            pltpu.VMEM((1, 8), jnp.float32),
+            pltpu.VMEM((1, 512), jnp.float32),
+            pltpu.VMEM((512, 4096), jnp.bfloat16),
+            pltpu.VMEM((24, 512, 128), jnp.bfloat16),
+            pltpu.VMEM((3, 24, 512), jnp.bfloat16),
+            pltpu.VMEM((3, 24, 128), jnp.bfloat16),
+            pltpu.VMEM((1, 24), jnp.int32),
+            pltpu.VMEM((1, 24), jnp.int32),
+            pltpu.VMEM((1, 24), jnp.int32),
+            pltpu.VMEM((192, 4096), jnp.bfloat16),
+            pltpu.VMEM((2048, 128), jnp.float32),
+            pltpu.VMEM((2048, 128), jnp.float32),
+            pltpu.VMEM((8, 192, 128), jnp.float32),
+            pltpu.VMEM((192, 128), jnp.float32),
+            pltpu.VMEM((192, 128), jnp.float32),
+            pltpu.VMEM((2, 8, 24, 128), jnp.float32),
+            pltpu.VMEM((192, 128), jnp.float32),
+            pltpu.VMEM((4, 192, 128), jnp.float32),
+            pltpu.VMEM((1248, 128), jnp.float32),
+            pltpu.VMEM((1248, 512), jnp.float32),
+            pltpu.VMEM((8, 24, 128), jnp.float32),
+            pltpu.VMEM((192, 512), jnp.float32),
+            pltpu.VMEM((512, 192), jnp.bfloat16),
+            pltpu.VMEM((192, 128), jnp.float32),
+            pltpu.VMEM((4, 192, 128), jnp.float32),
+            pltpu.VMEM((192, 512), jnp.bfloat16),
+            pltpu.VMEM((8, 24, 128), jnp.float32),
+            pltpu.VMEM((24, 128), jnp.float32),
+            pltpu.VMEM((24, 128), jnp.float32),
+            pltpu.VMEM((192, 128), jnp.float32),
             pltpu.VMEM((2, 4, 96, 1024), jnp.bfloat16),
-            half,
+            pltpu.VMEM((2, 6, 48, 1024), jnp.bfloat16),
             pltpu.VMEM((2, 2, 48, 1024), jnp.bfloat16),
             pltpu.VMEM((2, 4, 96, 256), jnp.bfloat16),
             pltpu.VMEM((2, 6, 48, 256), jnp.bfloat16),
@@ -273,28 +697,37 @@
             pltpu.SemaphoreType.DMA((4, 2, 6)),
             pltpu.SemaphoreType.DMA((8,)),
             pltpu.SemaphoreType.DMA((8,)),
+            pltpu.SemaphoreType.DMA((4,)),
+            pltpu.SemaphoreType.DMA((20,)),
+            pltpu.SemaphoreType.DMA((4,)),
         ],
         compiler_params=pltpu.CompilerParams(
-            collective_id=0, has_side_effects=True, vmem_limit_bytes=40 * 1024 * 1024
+            collective_id=0, has_side_effects=True, vmem_limit_bytes=38 * 1024 * 1024
         ),
-    )(rows, weight, counts)
-
-
-def convolve(window, fresh_rows, kernel, offset):
-    sequence = jnp.concatenate([window, fresh_rows], axis=1)
-    length = fresh_rows.shape[1]
-    summed = jnp.zeros(fresh_rows.shape, jnp.float32) + offset.astype(jnp.float32)
-    for tap_index in range(kernel.shape[0]):
-        summed = summed + kernel[tap_index].astype(jnp.float32) * sequence[
-            :, tap_index : tap_index + length
-        ].astype(jnp.float32)
-    return (jax.nn.silu(summed), sequence)
-
-
-def keep_window(sequence, kept_count, width_rows):
-    return jax.vmap(
-        lambda single, start_row: lax.dynamic_slice_in_dim(single, start_row, width_rows, 0)
-    )(sequence, kept_count)
+    )(*(pltpu.with_memory_space_constraint(operand, pltpu.HBM) for operand in operands))
+
+
+def place_kernel(*refs):
+    sources, targets, sems = refs[:4], refs[4:8], refs[8]
+    copies = [
+        pltpu.make_async_copy(source, target, sems.at[index])
+        for index, (source, target) in enumerate(zip(sources, targets))
+    ]
+    for copy in copies:
+        copy.start()
+    for copy in copies:
+        copy.wait()
+
+
+def place(*arrays):
+    return pl.pallas_call(
+        place_kernel,
+        out_shape=tuple(jax.ShapeDtypeStruct(a.shape, a.dtype) for a in arrays),
+        in_specs=[pl.BlockSpec(memory_space=pltpu.VMEM)] * 4,
+        out_specs=(pl.BlockSpec(memory_space=pltpu.HBM),) * 4,
+        scratch_shapes=[pltpu.SemaphoreType.DMA((4,))],
+        compiler_params=pltpu.CompilerParams(vmem_limit_bytes=16 * 1024 * 1024),
+    )(*arrays)
 
 
 def local(
@@ -319,90 +752,36 @@
     draft_lengths,
     live_flags,
 ):
-    requests, positions, model_width = tokens.shape
-    row_total = requests * positions
-    head_count = step_bias.shape[0]
-    inner_dev = value_offset.shape[0]
-    head_dim = inner_dev // head_count
-    tap_count = value_kernel.shape[0]
-    kept_count = accepted * live_flags
-    flat_rows = tokens.reshape(row_total, model_width).astype(jnp.float32)
-    normed = (
-        flat_rows
-        * lax.rsqrt(jnp.mean(flat_rows * flat_rows, axis=1, keepdims=True) + EPSILON)
-        * norm_gain
-    ).astype(jnp.bfloat16)
-    parity = lax.axis_index("tensor") % 2
-    in_flat = in_weight.reshape(in_weight.shape[0], 2 * inner_dev)
-    inner_sum = jnp.dot(normed, in_flat, preferred_element_type=jnp.float32)
-    group_sum = jnp.dot(normed, group_weight, preferred_element_type=jnp.float32)
-    step_raw = jnp.dot(normed, step_weight, preferred_element_type=jnp.float32)
-    inner_proj = inner_sum.astype(jnp.bfloat16).reshape(requests, positions, 2 * inner_dev)
-    gate_part = inner_proj[:, :, :inner_dev]
-    value_part = inner_proj[:, :, inner_dev:]
-    group_proj = group_sum.astype(jnp.bfloat16).reshape(requests, positions, group_weight.shape[1])
-    value_conv, value_seq = convolve(value_cache, value_part, value_kernel, value_offset)
-    own_conv, group_seq = convolve(group_cache, group_proj, group_kernel, group_offset)
-    other_conv = swapped(own_conv, "tensor", 0)
-    input_map = jnp.where(parity == 0, own_conv, other_conv)
-    output_map = jnp.where(parity == 0, other_conv, own_conv)
-    values = value_conv.reshape(requests, positions, head_count, head_dim)
-    step_size = jax.nn.softplus(step_raw.reshape(requests, positions, head_count) + step_bias)
-    log_decay = -step_size * decay_rate
-    prefix = jnp.concatenate(
-        [jnp.zeros((requests, 1, head_count), jnp.float32), jnp.cumsum(log_decay, axis=1)], axis=1
-    )
-    after_step = prefix[:, 1:]
-    alignment = jnp.einsum("rsn,rjn->rsj", output_map, input_map)
-    causal = (jnp.arange(positions)[:, None] >= jnp.arange(positions)[None, :])[None, :, :, None]
-    spread = after_step[:, :, None, :] - after_step[:, None, :, :]
-    weights_mix = (
-        jnp.where(causal, jnp.exp(jnp.where(causal, spread, 0.0)), 0.0)
-        * step_size[:, None, :, :]
-        * alignment[:, :, :, None]
-    )
-    within = jnp.einsum("rsjh,rjhp->rshp", weights_mix, values)
-    initial = scan_state.astype(jnp.float32)
-    carried = jnp.einsum("rhpn,rsn->rshp", initial, output_map) * jnp.exp(after_step)[:, :, :, None]
-    head_out = within + carried + skip_gain[:, None] * values
-    one_hot = (jnp.arange(positions + 1)[None, :] == kept_count[:, None]).astype(jnp.float32)
-    prefix_kept = jnp.sum(one_hot[:, :, None] * prefix, axis=1)
-    before_kept = (jnp.arange(positions)[None, :] < kept_count[:, None])[:, :, None]
-    keep_weight = (
-        jnp.where(
-            before_kept,
-            jnp.exp(jnp.where(before_kept, prefix_kept[:, None, :] - after_step, 0.0)),
-            0.0,
-        )
-        * step_size
-    )
-    weighted = keep_weight[:, :, :, None] * values
-    kept_state = (
-        jnp.exp(prefix_kept)[:, :, None, None] * initial
-        + jnp.einsum("rjhp,rjn->rhpn", weighted, input_map)
-    ).astype(jnp.bfloat16)
-    gated = head_out.reshape(row_total, inner_dev) * jax.nn.silu(
-        gate_part.reshape(row_total, inner_dev).astype(jnp.float32)
-    )
-    own_squares = jnp.sum(gated * gated, axis=1)
-    other_squares = swapped(own_squares, "tensor", 0)
-    scale_rows = lax.rsqrt((own_squares + other_squares) / (2 * inner_dev) + EPSILON)
-    valid_rows = (jnp.arange(positions)[None, :] < draft_lengths[:, None]) & (
-        live_flags[:, None] == 1
-    )
-    normalized = jnp.where(
-        valid_rows.reshape(row_total, 1), gated * scale_rows[:, None] * out_gain, 0.0
-    ).astype(jnp.bfloat16)
-    layer_rows, totals = exchange(normalized, out_weight, kept_count.reshape(1, requests))
-    accepted_total = totals[0, :1]
-    value_kept = keep_window(value_seq, kept_count, tap_count - 1)
-    group_kept = keep_window(group_seq, kept_count, tap_count - 1)
+    woven = in_weight.reshape(4096, 2, 4, 128).transpose(0, 2, 1, 3).reshape(32768, 128)
+    rows, kept_state, value_kept, group_kept, total = layer(
+        tokens.reshape(192, 4096),
+        norm_gain.reshape(1, 4096),
+        woven,
+        group_weight,
+        step_weight.T,
+        value_kernel,
+        value_offset,
+        group_kernel,
+        group_offset,
+        step_bias.reshape(1, 8),
+        decay_rate.reshape(1, 8),
+        skip_gain.reshape(1, 8),
+        out_gain.reshape(1, 512),
+        out_weight,
+        scan_state.reshape(24, 512, 128),
+        value_cache.transpose(1, 0, 2),
+        group_cache.transpose(1, 0, 2),
+        accepted.reshape(1, 24),
+        draft_lengths.reshape(1, 24),
+        live_flags.reshape(1, 24),
+    )
+    rows, kept_state, value_kept, group_kept = place(rows, kept_state, value_kept, group_kept)
     return (
-        layer_rows.reshape(requests, positions, model_width),
-        kept_state,
-        value_kept,
-        group_kept,
-        accepted_total,
+        rows.reshape(24, 8, 4096),
+        kept_state.reshape(24, 8, 64, 128),
+        value_kept.transpose(1, 0, 2),
+        group_kept.transpose(1, 0, 2),
+        total,
     )
 
 

time: 95.6 us -> 61.2 us (0.64)
  local copies, waits for them, and re-layouts: 22.6 us -> 0 us
  matrix products: 21.9 us -> 0 us
  Pallas kernels: 41 us -> 58.6 us
  other arithmetic: 6.14 us -> 0 us
  starting transfers between devices: 2.37 us -> 0 us
  between operations: 1.03 us -> 2.41 us
    dot_general x7 -> x0, matrix products: 21.9 us -> none  [the longest x1 5.55 us: local(): jnp.einsum('rhpn,rsn->rshp', initial, output_map)]
    pallas_call x1 -> x2, Pallas kernels: 41 us -> 58.6 us  [the longest x1 56.4 us: layer(): pl.pallas_call(layer_kernel, out_shape=(jax.ShapeDtypeStruct((192, 4096),...]
    unnamed x38 -> x0, local copies, waits for them, and re-layouts: 13.6 us -> none
    gather x2 -> x0, local copies, waits for them, and re-layouts: 3.05 us -> none  [keep_window(): lax.dynamic_slice_in_dim(single, start_row, width_rows, 0)]
    ppermute x2 -> x0, starting transfers between devices: 2.37 us -> none  [swapped(): return lax.ppermute(value, axis, pairs)]
    reduce_sum x2 -> x0, other arithmetic: 2.01 us -> none  [the longest x1 1.88 us: local(): jnp.mean(flat_rows * flat_rows, axis=1, keepdims=True) + EPSILON]
    convert_element_type x7 -> x0, other arithmetic: 1.79 us -> none  [the longest x2 0.84 us: convolve(): kernel[tap_index].astype(jnp.float32)]
    select_n x1 -> x0, local copies, waits for them, and re-layouts: 1.63 us -> none  [local(): jax.nn.softplus(step_raw.reshape(requests, positions, head_count) + step_...]
  transfers between devices with their start and end apart: 2 -> 0, of which waited for: 0 -> 0; matrix products, arithmetic and copies ran while one was open for 34% -> 0% of each run, Pallas kernels for 0% -> 0%
where the time goes in v2:
time: 61.2 us; the launch traced here: 61.1 us
  Pallas kernels  58.6 us (96%)
  between operations  2.41 us (4%)
    pallas_call x1, Pallas kernels, layer(): pl.pallas_call(layer_kernel, out_shape=(jax.ShapeDtypeStruct((192, 4096),...  56.4 us
    pallas_call x1, Pallas kernels, place(): pl.pallas_call(place_kernel, out_shape=tuple((jax.ShapeDtypeStruct(a.shap...  2.23 us

profile of v2, /device:TPU:0, one launch (start us, length us, event | category | flops | bytes accessed | tf_op | source)
XLA Modules:
  0.0 61.1 jit_solution(6170783716709571006)
XLA Ops:
  0.6 56.4 %shard_map.227 = (bf16[192,4096]{1,0:T(8,128)(2,1)S(1)}, bf16[24,512,128]{2,1,0:T(8,128)(2,1)S(1)}, bf16[3,24,512]{2,1,0:T(8,128)(2,1)S(1)}, bf16[3,24,128]{2,1,0:T(8,128)(2,1)S(1)}, s32[1]{0:T(128)}) custom-call(bf16[192,4096]{1,0:T(8,128)(2,1)} %bitcast.24, f32[1,4096]{1,0:T(1,128)} %bitcast.28, bf16[32768,128]{1,0:T(8,128)(2,1)} %bitcast.22, ...), custom_call_target="tpu_custom_call" | custom-call | tf_op jit(solution)/shard_map/pallas_call | solution.py:635
  57.1 2.2 %shard_map.228 = (bf16[192,4096]{1,0:T(8,128)(2,1)}, bf16[24,512,128]{2,1,0:T(8,128)(2,1)}, bf16[3,24,512]{2,1,0:T(8,128)(2,1)}, bf16[3,24,128]{2,1,0:T(8,128)(2,1)}) custom-call(bf16[192,4096]{1,0:T(8,128)(2,1)S(1)} %get-tuple-element.14.refs_0_, bf16[24,512,128]{2,1,0:T(8,128)(2,1)S(1)} %get-tuple-element.15.refs_1_, ...), custom_call_target="tpu_custom_call" | custom-call | tf_op jit(solution)/shard_map/pallas_call | solution.py:723

commit v3 on v2

--- a/solution.py
+++ b/solution.py
@@ -115,12 +115,11 @@
     square_own,
     square_other,
     scale_rows,
+    first_products,
     partial,
     first_recv,
     first_mix,
-    first_sum,
-    second_recv,
-    second_mix,
+    gathered,
     count_buf,
     send_sems,
     recv_sems,
@@ -128,6 +127,7 @@
     count_recv,
     swap_sems,
     load_sems,
+    token_sems,
     chunk_sems,
 ):
     z, y, along_z, along_y = ring_places()
@@ -145,25 +145,28 @@
         loads[name] = pltpu.make_async_copy(src, dst, load_sems.at[index])
         loads[name].start()
 
-    load("tokens", tokens_in, tokens, 0)
+    token_copies = []
+    for index in range(4):
+        rows = pl.ds(index * 48, 48)
+        copy = pltpu.make_async_copy(tokens_in.at[rows], tokens.at[rows], token_sems.at[index])
+        copy.start()
+        token_copies.append(copy)
     load("gain", gain_in, gain, 1)
-    load("group_weight", group_weight_in, group_weight, 3)
+    load("step_weight", step_weight_in, step_weight, 4)
+    load("group_weight", group_weight_in, group_weight.at[:, 0:128], 3)
     load("accepted", accepted_in, accepted, 17)
     load("lengths", lengths_in, lengths, 18)
     load("live", live_in, live, 19)
     load("group_cache", group_cache_in, group_cache, 16)
     load("group_kernel", group_kernel_in, group_kernel, 7)
     load("group_offset", group_offset_in, group_offset, 8)
-    load("step_weight", step_weight_in, step_weight, 4)
     load("step_bias", step_bias_in, step_bias, 9)
     load("decay_rate", decay_rate_in, decay_rate, 10)
     load("skip_gain", skip_gain_in, skip_gain, 11)
-    chunks = []
     for index in range(4):
         rows = pl.ds(index * 8192, 8192)
         copy = pltpu.make_async_copy(in_weight_in.at[rows], in_weight.at[rows], chunk_sems.at[index])
         copy.start()
-        chunks.append(copy)
     load("value_cache", value_cache_in, value_cache, 15)
     load("value_kernel", value_kernel_in, value_kernel, 5)
     load("value_offset", value_offset_in, value_offset, 6)
@@ -177,11 +180,16 @@
         values = jnp.broadcast_to(ref[...].astype(jnp.float32), (24, 24))
         return jnp.sum(jnp.where(square, values, 0.0), axis=1, keepdims=True)
 
+    loads["step_weight"].wait()
+    for block in range(32):
+        rows = slice(block * 128, (block + 1) * 128)
+        group_weight[rows, 128:136] = jnp.transpose(
+            step_weight[:, rows].astype(jnp.float32)
+        ).astype(jnp.bfloat16)
     loads["gain"].wait()
-    loads["tokens"].wait()
-
-    def normalize(block, carry):
-        rows = pl.ds(pl.multiple_of(block * 16, 16), 16)
+
+    def normalize(block):
+        rows = slice(block * 16, block * 16 + 16)
         total = jnp.zeros((16, 256), jnp.float32)
         for part in range(16):
             piece = tokens[rows, part * 256 : (part + 1) * 256].astype(jnp.float32)
@@ -192,13 +200,15 @@
             columns = slice(part * 256, (part + 1) * 256)
             piece = tokens[rows, columns].astype(jnp.float32)
             normed[rows, columns] = (piece * scale * gain[:, columns]).astype(jnp.bfloat16)
-        return carry
-
-    lax.fori_loop(0, 12, normalize, 0)
+
+    for index in range(4):
+        token_copies[index].wait()
+        for block in range(3):
+            normalize(index * 3 + block)
     loads["group_weight"].wait()
-    group_rows[...] = jnp.dot(
-        normed[...], group_weight[...], preferred_element_type=jnp.float32
-    )
+    product = jnp.dot(normed[...], group_weight[...], preferred_element_type=jnp.float32)
+    group_rows[...] = product[:, 0:128]
+    step_rows[...] = product[:, 128:256]
     for name in ("accepted", "lengths", "live", "group_cache", "group_kernel", "group_offset"):
         loads[name].wait()
     kept = column(accepted) * column(live)
@@ -255,29 +265,23 @@
     for t in range(3):
         group_kept[t] = kept_rows(group_sequence, kept, t)
 
-    for name in ("step_weight", "step_bias", "decay_rate", "skip_gain"):
+    for name in ("step_bias", "decay_rate", "skip_gain"):
         loads[name].wait()
-    step_rows[:, 0:8] = lax.dot_general(
-        normed[...],
-        step_weight[...],
-        (((1,), (1,)), ((), ())),
-        preferred_element_type=jnp.float32,
-    )
 
     inner[...] = jnp.zeros_like(inner)
 
     def widen(start, spread):
-        spread[...] = in_weight[pl.ds(pl.multiple_of(start * 2048, 2048), 2048), :].astype(
+        spread[...] = in_weight[pl.ds(pl.multiple_of(start * 4096, 4096), 4096), :].astype(
             jnp.float32
         )
 
     def multiply(start, spread):
-        left = normed[:, pl.ds(pl.multiple_of(start * 256, 256), 256)]
+        left = normed[:, pl.ds(pl.multiple_of(start * 512, 512), 512)]
         for part in range(2):
             for j in range(0, 4, 2):
                 right = jnp.concatenate(
                     [
-                        spread[pl.ds((j + i) * 2 + part, 256, stride=8), :].astype(jnp.bfloat16)
+                        spread[pl.ds((j + i) * 2 + part, 512, stride=8), :].astype(jnp.bfloat16)
                         for i in range(2)
                     ],
                     axis=1,
@@ -287,15 +291,17 @@
                     inner[part * 4 + j + i] += product[:, i * 128 : (i + 1) * 128]
 
     def pair(index, carry):
+        rows = pl.ds(pl.multiple_of(index * 8192, 8192), 8192)
+        pltpu.make_async_copy(
+            in_weight_in.at[rows], in_weight.at[rows], chunk_sems.at[index]
+        ).wait()
         widen(2 * index, spread_a)
         multiply(2 * index, spread_a)
         widen(2 * index + 1, spread_b)
         multiply(2 * index + 1, spread_b)
         return carry
 
-    for index in range(4):
-        chunks[index].wait()
-        lax.fori_loop(2 * index, 2 * index + 2, pair, 0)
+    lax.fori_loop(0, 4, pair, 0)
 
     steps, after = [], []
     running = None
@@ -332,18 +338,19 @@
     ).astype(jnp.bfloat16)
 
     def expand(index, carry):
-        rows = pl.ds(pl.multiple_of(index * 208, 16), 208)
+        rows = pl.ds(index * 416, 416)
         mixing[rows, :] = jnp.dot(
             small[rows, 0:8].astype(jnp.bfloat16), hot, preferred_element_type=jnp.float32
         )
         return carry
 
-    lax.fori_loop(0, 6, expand, 0)
+    for index in range(3):
+        expand(index, 0)
     loads["state"].wait()
 
     def carry_over(index, carry):
-        for i in range(6):
-            request = index * 6 + i
+        for i in range(12):
+            request = index * 12 + i
             rows = pl.ds(pl.multiple_of(request * 8, 8), 8)
             product = lax.dot_general(
                 map_rows[rows, :].astype(jnp.bfloat16),
@@ -355,7 +362,7 @@
                 carried[block, rows, :] = product[:, block * 128 : (block + 1) * 128]
         return carry
 
-    lax.fori_loop(0, 4, carry_over, 0)
+    lax.fori_loop(0, 2, carry_over, 0)
     for name in ("value_cache", "value_kernel", "value_offset", "out_gain"):
         loads[name].wait()
 
@@ -422,14 +429,42 @@
     for block in range(4):
         rows_ref[:, block * 128 : (block + 1) * 128] = gated_rows[block].astype(jnp.bfloat16)
     loads["out_weight"].wait()
-    weight_ref = out_weight
+    firsts = [along_y, along_z]
+    seconds = [along_z, along_y]
+    first_at = [y, z]
+    second_at = [z, y]
+    copies = []
+
+    def launch(src, dst, stage, route, chunk, slot, place):
+        copy = remote(src, dst, (send_sems, recv_sems, (stage, route, chunk, slot)), place)
+        copy.start()
+        copies.append(copy)
+        return copy
+
+    def product_of(route, step, chunk):
+        base = ((first_at[route] + step) % 4) * 1024 + chunk * 512
+        return jnp.dot(
+            rows_ref[pl.ds(route * 96, 96), :],
+            out_weight[:, pl.ds(pl.multiple_of(base, 512), 512)],
+            preferred_element_type=jnp.float32,
+        )
+
+    def settle(route, step, chunk, product):
+        scale = scale_rows[pl.ds(route * 96, 96), :]
+        partial[route, step, chunk] = (
+            product * jnp.concatenate([scale] * 4, axis=1)
+        ).astype(jnp.bfloat16)
+
+    for step in (2, 1, 3):
+        for route in range(2):
+            first_products[route, step - 1] = product_of(route, step, 0)
     turned[...] = jnp.transpose(weighted[...]).astype(jnp.bfloat16)
     square_swap.wait_recv()
     scales = lax.rsqrt((square_own[...] + square_other[...]) / 1024.0 + EPSILON)
     for s in range(8):
         scale_rows[pl.ds(s, 24, stride=8), :] = jnp.broadcast_to(scales[:, s : s + 1], (24, 128))
 
-    def keep_states():
+    def keep_states(first, last):
         owner = lax.rem(lax.broadcasted_iota(jnp.int32, (192, 128), 0), 24)
 
         def keep(index, carry):
@@ -454,173 +489,110 @@
                     ).astype(jnp.bfloat16)
             return carry
 
-        lax.fori_loop(0, 12, keep, 0)
-
-    firsts = [along_y, along_z]
-    seconds = [along_z, along_y]
-    first_at = [y, z]
-    second_at = [z, y]
-    copies = []
-
-    def launch(src, dst, stage, route, slot, place):
-        copy = remote(src, dst, (send_sems, recv_sems, (stage, route, slot)), place)
-        copy.start()
-        copies.append(copy)
-        return copy
-
-    def project(route, step):
-        base = ((first_at[route] + step) % 4) * 1024
-
-        def one(j, carry):
-            columns = pl.ds(pl.multiple_of(base + j * 256, 256), 256)
-            product = jnp.dot(
-                rows_ref[pl.ds(route * 96, 96), :],
-                weight_ref[:, columns],
-                preferred_element_type=jnp.float32,
-            )
-            scale = scale_rows[pl.ds(route * 96, 96), :]
-            partial[route, step, :, pl.ds(pl.multiple_of(j * 256, 256), 256)] = (
-                product * jnp.concatenate([scale, scale], axis=1)
-            ).astype(jnp.bfloat16)
-            return carry
-
-        lax.fori_loop(0, 4, one, 0)
-
-    project(0, 2)
-
-    def first_step(route):
-        unit = partial.at[route]
-        plus, minus = (firsts[route][1], firsts[route][3])
-        a = launch(unit.at[2, TOP], first_recv.at[route, 0], 0, route, 0, plus)
-        b = launch(unit.at[2, BOTTOM], first_recv.at[route, 1], 0, route, 1, minus)
-        return [a, b]
-
-    held = [first_step(0)]
-    project(1, 2)
-    held.append(first_step(1))
-    for route in range(2):
-        project(route, 1)
-        held[route].append(
-            launch(
-                partial.at[route, 1, BOTTOM], first_recv.at[route, 3], 0, route, 3, firsts[route][1]
-            )
-        )
-    for route in range(2):
-        project(route, 3)
-        held[route].append(
-            launch(
-                partial.at[route, 3, TOP], first_recv.at[route, 4], 0, route, 4, firsts[route][3]
-            )
-        )
-    for route in range(2):
-        held[route][0].wait_recv()
-        first_mix[route, 0] = widened_sum(first_recv.at[route, 0], partial.at[route, 1, TOP])
-        held[route].append(
-            launch(first_mix.at[route, 0], first_recv.at[route, 2], 0, route, 2, firsts[route][1])
-        )
-        held[route][1].wait_recv()
-        first_mix[route, 1] = widened_sum(first_recv.at[route, 1], partial.at[route, 3, BOTTOM])
-        held[route].append(
-            launch(first_mix.at[route, 1], first_recv.at[route, 5], 0, route, 5, firsts[route][3])
-        )
-    for route in range(2):
-        project(route, 0)
-    keep_states()
-    for half in range(2):
+        lax.fori_loop(first, last, keep, 0)
+
+    held = {}
+    for chunk in range(2):
+        for step in (2, 1, 3):
+            for route in range(2):
+                product = first_products[route, step - 1] if chunk == 0 else product_of(route, step, 1)
+                settle(route, step, chunk, product)
+                unit = partial.at[route, step, chunk]
+                landing = first_recv.at[route, chunk]
+                plus, minus = (firsts[route][1], firsts[route][3])
+                sends = {
+                    2: ((TOP, 0, plus), (BOTTOM, 1, minus)),
+                    1: ((BOTTOM, 3, plus),),
+                    3: ((TOP, 4, minus),),
+                }[step]
+                for rows, slot, place in sends:
+                    held[route, chunk, slot] = launch(
+                        unit.at[rows], landing.at[slot], 0, route, chunk, slot, place
+                    )
+    for chunk in range(2):
         for route in range(2):
-            rows = (TOP, BOTTOM)[half]
-            waits = ((3, 4), (2, 5))[half]
-            for index in waits:
-                held[route][index].wait_recv()
-            plus_ref = first_recv.at[route, 2 + half]
-            minus_ref = first_recv.at[route, 4 + half]
-            for j in range(4):
-                columns = pl.ds(j * 256, 256)
-                first_sum[route, j, rows] = widened_sum(
-                    partial.at[route, 0, rows, columns],
-                    plus_ref.at[:, columns],
-                    minus_ref.at[:, columns],
-                )
-    late = []
-    for route in range(2):
-        at = second_at[route]
-        plus, minus = (seconds[route][1], seconds[route][3])
-        unit = [first_sum.at[route, (at + k) % 4] for k in range(4)]
-        landing = second_recv.at[route]
-        late.append(
-            [
-                launch(unit[2].at[TOP], landing.at[0], 1, route, 0, plus),
-                launch(unit[2].at[BOTTOM], landing.at[1], 1, route, 1, minus),
-                launch(unit[1].at[BOTTOM], landing.at[3], 1, route, 3, plus),
-                launch(unit[3].at[TOP], landing.at[4], 1, route, 4, minus),
-            ]
-        )
-    for route in range(2):
-        at = second_at[route]
-        plus, minus = (seconds[route][1], seconds[route][3])
-        landing = second_recv.at[route]
-        late[route][0].wait_recv()
-        second_mix[route, 0] = widened_sum(landing.at[0], first_sum.at[route, (at + 1) % 4, TOP])
-        late[route].append(
-            launch(second_mix.at[route, 0], landing.at[2], 1, route, 2, plus)
-        )
-        late[route][1].wait_recv()
-        second_mix[route, 1] = widened_sum(landing.at[1], first_sum.at[route, (at + 3) % 4, BOTTOM])
-        late[route].append(
-            launch(second_mix.at[route, 1], landing.at[5], 1, route, 5, minus)
-        )
-
-    def spot(route, half, first, second, width):
-        column = pl.multiple_of(first * 1024 + second * 256, 256)
-        return out_ref.at[pl.ds(route * 96 + half * 48, 48), pl.ds(column, width)]
-
-    for half in range(2):
-        for route in range(2):
-            rows = (TOP, BOTTOM)[half]
-            waits = ((3, 4), (2, 5))[half]
-            for index in waits:
-                late[route][index].wait_recv()
-            own = spot(route, half, first_at[route], second_at[route], 256)
-            own[...] = widened_sum(
-                first_sum.at[route, second_at[route], rows],
-                second_recv.at[route, 2 + half],
-                second_recv.at[route, 4 + half],
-            )
-
-    def spread(stage, places, piece):
+            settle(route, 0, chunk, product_of(route, 0, chunk))
+    for chunk in range(2):
+        for half in range(2):
+            for route in range(2):
+                rows = (TOP, BOTTOM)[half]
+                landing = first_recv.at[route, chunk]
+                held[route, chunk, half].wait_recv()
+                mix = first_mix.at[route, chunk, half]
+                mix[...] = widened_sum(
+                    landing.at[half], partial.at[route, (1, 3)[half], chunk, rows]
+                )
+                slot = (2, 5)[half]
+                held[route, chunk, slot] = launch(
+                    mix, landing.at[slot], 0, route, chunk, slot, firsts[route][(1, 3)[half]]
+                )
+
+    def spread_start(stage, places, piece, chunk):
         started = []
         for route in range(2):
             plus, minus = (places[route][1], places[route][3])
-            started.append(
-                [
-                    launch(piece(route, 0, 0), piece(route, 0, 0), stage, route, 0, plus),
-                    launch(piece(route, 1, 0), piece(route, 1, 0), stage, route, 1, minus),
-                    launch(piece(route, 1, 0), piece(route, 1, 0), stage, route, 2, plus),
-                    launch(piece(route, 0, 0), piece(route, 0, 0), stage, route, 3, minus),
-                ]
-            )
-        for route in range(2):
-            plus, minus = (places[route][1], places[route][3])
-            started[route][0].wait_recv()
-            started[route].append(
-                launch(piece(route, 0, 3), piece(route, 0, 3), stage, route, 4, plus)
-            )
-            started[route][1].wait_recv()
-            started[route].append(
-                launch(piece(route, 1, 1), piece(route, 1, 1), stage, route, 5, minus)
-            )
+            started.append([])
+            for half, slot, place in ((0, 0, plus), (1, 1, minus), (1, 2, plus), (0, 3, minus)):
+                own = piece(route, chunk, half, 0)
+                started[route].append(launch(own, own, stage, route, chunk, slot, place))
+        return started
+
+    def spread_forward(started, stage, places, piece, chunk):
+        for half in range(2):
+            for route in range(2):
+                started[route][half].wait_recv()
+                passed = piece(route, chunk, half, (3, 1)[half])
+                started[route].append(
+                    launch(
+                        passed, passed, stage, route, chunk, 4 + half, places[route][(1, 3)[half]]
+                    )
+                )
+
+    def spread_finish(started):
         for route in range(2):
             for index in range(2, 6):
                 started[route][index].wait_recv()
 
-    def near(route, half, k):
-        return spot(route, half, first_at[route], (second_at[route] + k) % 4, 256)
-
-    def far(route, half, k):
-        return spot(route, half, (first_at[route] + k) % 4, 0, 1024)
-
-    spread(2, seconds, near)
-    spread(3, firsts, far)
+    def middle(route, chunk, half, k):
+        return gathered.at[route, chunk, (second_at[route] + k) % 4, (TOP, BOTTOM)[half]]
+
+    def spot(route, chunk, half, k):
+        column = ((first_at[route] + k) % 4) * 1024 + chunk * 512
+        return out_ref.at[
+            pl.ds(route * 96 + half * 48, 48), pl.ds(pl.multiple_of(column, 512), 512)
+        ]
+
+    inner_spread = []
+    for chunk in range(2):
+        for half in range(2):
+            for route in range(2):
+                rows = (TOP, BOTTOM)[half]
+                for slot in ((4, 2), (3, 5))[half]:
+                    held[route, chunk, slot].wait_recv()
+                own = middle(route, chunk, half, 0)
+                own[...] = widened_sum(
+                    partial.at[route, 0, chunk, rows],
+                    first_recv.at[route, chunk, 2 + half],
+                    first_recv.at[route, chunk, 4 + half],
+                )
+        inner_spread.append(spread_start(1, seconds, middle, chunk))
+    keep_states(0, 6)
+    for chunk in range(2):
+        spread_forward(inner_spread[chunk], 1, seconds, middle, chunk)
+    outer_spread = []
+    for chunk in range(2):
+        spread_finish(inner_spread[chunk])
+        for half in range(2):
+            for route in range(2):
+                rows = (TOP, BOTTOM)[half]
+                own = spot(route, chunk, half, 0)
+                own[...] = widened_sum(*(gathered.at[route, chunk, b, rows] for b in range(4)))
+        outer_spread.append(spread_start(2, firsts, spot, chunk))
+    keep_states(6, 12)
+    for chunk in range(2):
+        spread_forward(outer_spread[chunk], 2, firsts, spot, chunk)
+    for chunk in range(2):
+        spread_finish(outer_spread[chunk])
     for copy in count_copies:
         copy.wait_recv()
     everyone = count_buf[0]
@@ -648,7 +620,7 @@
             pltpu.VMEM((192, 4096), jnp.bfloat16),
             pltpu.VMEM((1, 4096), jnp.float32),
             pltpu.VMEM((32768, 128), jnp.bfloat16),
-            pltpu.VMEM((4096, 128), jnp.bfloat16),
+            pltpu.VMEM((4096, 256), jnp.bfloat16),
             pltpu.VMEM((8, 4096), jnp.bfloat16),
             pltpu.VMEM((4, 512), jnp.bfloat16),
             pltpu.VMEM((512,), jnp.bfloat16),
@@ -666,8 +638,8 @@
             pltpu.VMEM((1, 24), jnp.int32),
             pltpu.VMEM((1, 24), jnp.int32),
             pltpu.VMEM((192, 4096), jnp.bfloat16),
-            pltpu.VMEM((2048, 128), jnp.float32),
-            pltpu.VMEM((2048, 128), jnp.float32),
+            pltpu.VMEM((4096, 128), jnp.float32),
+            pltpu.VMEM((4096, 128), jnp.float32),
             pltpu.VMEM((8, 192, 128), jnp.float32),
             pltpu.VMEM((192, 128), jnp.float32),
             pltpu.VMEM((192, 128), jnp.float32),
@@ -686,23 +658,23 @@
             pltpu.VMEM((24, 128), jnp.float32),
             pltpu.VMEM((24, 128), jnp.float32),
             pltpu.VMEM((192, 128), jnp.float32),
-            pltpu.VMEM((2, 4, 96, 1024), jnp.bfloat16),
-            pltpu.VMEM((2, 6, 48, 1024), jnp.bfloat16),
-            pltpu.VMEM((2, 2, 48, 1024), jnp.bfloat16),
-            pltpu.VMEM((2, 4, 96, 256), jnp.bfloat16),
-            pltpu.VMEM((2, 6, 48, 256), jnp.bfloat16),
-            pltpu.VMEM((2, 2, 48, 256), jnp.bfloat16),
+            pltpu.VMEM((2, 3, 96, 512), jnp.float32),
+            pltpu.VMEM((2, 4, 2, 96, 512), jnp.bfloat16),
+            pltpu.VMEM((2, 2, 6, 48, 512), jnp.bfloat16),
+            pltpu.VMEM((2, 2, 2, 48, 512), jnp.bfloat16),
+            pltpu.VMEM((2, 2, 4, 96, 512), jnp.bfloat16),
             pltpu.VMEM((8, 8, 128), jnp.float32),
-            pltpu.SemaphoreType.DMA((4, 2, 6)),
-            pltpu.SemaphoreType.DMA((4, 2, 6)),
+            pltpu.SemaphoreType.DMA((3, 2, 2, 6)),
+            pltpu.SemaphoreType.DMA((3, 2, 2, 6)),
             pltpu.SemaphoreType.DMA((8,)),
             pltpu.SemaphoreType.DMA((8,)),
             pltpu.SemaphoreType.DMA((4,)),
             pltpu.SemaphoreType.DMA((20,)),
             pltpu.SemaphoreType.DMA((4,)),
+            pltpu.SemaphoreType.DMA((4,)),
         ],
         compiler_params=pltpu.CompilerParams(
-            collective_id=0, has_side_effects=True, vmem_limit_bytes=38 * 1024 * 1024
+            collective_id=0, has_side_effects=True, vmem_limit_bytes=44 * 1024 * 1024
         ),
     )(*(pltpu.with_memory_space_constraint(operand, pltpu.HBM) for operand in operands))
 

time: 61.2 us -> 51.1 us (0.83)
  Pallas kernels: 58.6 us -> 48.6 us
    pallas_call x1, Pallas kernels: 56.4 us -> 46.4 us  [layer(): pl.pallas_call(layer_kernel, out_shape=(jax.ShapeDtypeStruct((192, 4096),...]
where the time goes in v3:
time: 51.1 us; the launch traced here: 51 us
  Pallas kernels  48.6 us (95%)
  between operations  2.41 us (5%)
    pallas_call x1, Pallas kernels, layer(): pl.pallas_call(layer_kernel, out_shape=(jax.ShapeDtypeStruct((192, 4096),...  46.4 us
    pallas_call x1, Pallas kernels, place(): pl.pallas_call(place_kernel, out_shape=tuple((jax.ShapeDtypeStruct(a.shap...  2.23 us

profile of v3, /device:TPU:0, one launch (start us, length us, event | category | flops | bytes accessed | tf_op | source)
XLA Modules:
  0.0 51.0 jit_solution(7352295797767210258)
XLA Ops:
  0.6 46.4 %shard_map.227 = (bf16[192,4096]{1,0:T(8,128)(2,1)S(1)}, bf16[24,512,128]{2,1,0:T(8,128)(2,1)S(1)}, bf16[3,24,512]{2,1,0:T(8,128)(2,1)S(1)}, bf16[3,24,128]{2,1,0:T(8,128)(2,1)S(1)}, s32[1]{0:T(128)}) custom-call(bf16[192,4096]{1,0:T(8,128)(2,1)} %bitcast.24, f32[1,4096]{1,0:T(1,128)} %bitcast.28, bf16[32768,128]{1,0:T(8,128)(2,1)} %bitcast.22, ...), custom_call_target="tpu_custom_call" | custom-call | tf_op jit(solution)/shard_map/pallas_call | solution.py:607
  47.0 2.2 %shard_map.228 = (bf16[192,4096]{1,0:T(8,128)(2,1)}, bf16[24,512,128]{2,1,0:T(8,128)(2,1)}, bf16[3,24,512]{2,1,0:T(8,128)(2,1)}, bf16[3,24,128]{2,1,0:T(8,128)(2,1)}) custom-call(bf16[192,4096]{1,0:T(8,128)(2,1)S(1)} %get-tuple-element.14.refs_0_, bf16[24,512,128]{2,1,0:T(8,128)(2,1)S(1)} %get-tuple-element.15.refs_1_, ...), custom_call_target="tpu_custom_call" | custom-call | tf_op jit(solution)/shard_map/pallas_call | solution.py:695

commit v4 on v3

--- a/solution.py
+++ b/solution.py
@@ -18,7 +18,7 @@
 
 
 MESH = pl.DeviceIdType.MESH
-TOP, BOTTOM = pl.ds(0, 48), pl.ds(48, 48)
+HALVES = (pl.ds(0, 512), pl.ds(512, 512))
 
 
 def ring_places():
@@ -29,13 +29,12 @@
     return (z, y, along_z, along_y)
 
 
-def remote(src, dst, sems, place):
-    send, recv, index = sems
+def remote(src, dst, send, recv, place):
     return pltpu.make_async_remote_copy(
         src_ref=src,
         dst_ref=dst,
-        send_sem=send.at[index],
-        recv_sem=recv.at[index],
+        send_sem=send,
+        recv_sem=recv,
         device_id=place,
         device_id_type=MESH,
     )
@@ -121,10 +120,10 @@
     first_mix,
     gathered,
     count_buf,
+    total_own,
     send_sems,
     recv_sems,
-    count_send,
-    count_recv,
+    count_sems,
     swap_sems,
     load_sems,
     token_sems,
@@ -163,16 +162,10 @@
     load("step_bias", step_bias_in, step_bias, 9)
     load("decay_rate", decay_rate_in, decay_rate, 10)
     load("skip_gain", skip_gain_in, skip_gain, 11)
-    for index in range(4):
+    def load_chunk(index):
         rows = pl.ds(index * 8192, 8192)
-        copy = pltpu.make_async_copy(in_weight_in.at[rows], in_weight.at[rows], chunk_sems.at[index])
-        copy.start()
-    load("value_cache", value_cache_in, value_cache, 15)
-    load("value_kernel", value_kernel_in, value_kernel, 5)
-    load("value_offset", value_offset_in, value_offset, 6)
-    load("out_gain", out_gain_in, out_gain, 12)
-    load("state", state_in, state, 14)
-    load("out_weight", out_weight_in, out_weight, 13)
+        pltpu.make_async_copy(in_weight_in.at[rows], in_weight.at[rows], chunk_sems.at[index]).start()
+
     def column(ref):
         square = lax.broadcasted_iota(jnp.int32, (24, 24), 0) == lax.broadcasted_iota(
             jnp.int32, (24, 24), 1
@@ -203,8 +196,17 @@
 
     for index in range(4):
         token_copies[index].wait()
+        if index in (1, 3):
+            load_chunk(index - 1)
+            load_chunk(index)
         for block in range(3):
             normalize(index * 3 + block)
+    load("value_cache", value_cache_in, value_cache, 15)
+    load("value_kernel", value_kernel_in, value_kernel, 5)
+    load("value_offset", value_offset_in, value_offset, 6)
+    load("out_gain", out_gain_in, out_gain, 12)
+    load("state", state_in, state, 14)
+    load("out_weight", out_weight_in, out_weight, 13)
     loads["group_weight"].wait()
     product = jnp.dot(normed[...], group_weight[...], preferred_element_type=jnp.float32)
     group_rows[...] = product[:, 0:128]
@@ -257,11 +259,10 @@
     )
     swap.start()
     count_buf[0] = jnp.broadcast_to(jnp.sum(kept, axis=0, keepdims=True), (8, 128))
-    count_copies = []
     for d in range(1, 8):
-        copy = remote(count_buf.at[0], count_buf.at[d], (count_send, count_recv, d), dp_peers[d - 1])
-        copy.start()
-        count_copies.append(copy)
+        remote(
+            count_buf.at[0], count_buf.at[d], count_sems.at[0], count_sems.at[1], dp_peers[d - 1]
+        ).start()
     for t in range(3):
         group_kept[t] = kept_rows(group_sequence, kept, t)
 
@@ -290,18 +291,26 @@
                 for i in range(2):
                     inner[part * 4 + j + i] += product[:, i * 128 : (i + 1) * 128]
 
-    def pair(index, carry):
+    def await_chunk(index):
         rows = pl.ds(pl.multiple_of(index * 8192, 8192), 8192)
         pltpu.make_async_copy(
             in_weight_in.at[rows], in_weight.at[rows], chunk_sems.at[index]
         ).wait()
-        widen(2 * index, spread_a)
+
+    def pair(index, carry):
+        await_chunk(index + 1)
         multiply(2 * index, spread_a)
         widen(2 * index + 1, spread_b)
         multiply(2 * index + 1, spread_b)
+        widen(2 * index + 2, spread_a)
         return carry
 
-    lax.fori_loop(0, 4, pair, 0)
+    await_chunk(0)
+    widen(0, spread_a)
+    lax.fori_loop(0, 3, pair, 0)
+    multiply(6, spread_a)
+    widen(7, spread_b)
+    multiply(7, spread_b)
 
     steps, after = [], []
     running = None
@@ -348,10 +357,15 @@
         expand(index, 0)
     loads["state"].wait()
 
-    def carry_over(index, carry):
-        for i in range(12):
-            request = index * 12 + i
-            rows = pl.ds(pl.multiple_of(request * 8, 8), 8)
+    for name in ("value_cache", "value_kernel", "value_offset", "out_gain"):
+        loads[name].wait()
+    offset_row = value_offset[...].astype(jnp.float32).reshape(1, 512)
+    lane = lax.broadcasted_iota(jnp.int32, (8, 128), 1)
+    square_copies = []
+    for tile in range(3):
+        eight = pl.ds(tile * 8, 8)
+        for request in range(tile * 8, tile * 8 + 8):
+            rows = pl.ds(request * 8, 8)
             product = lax.dot_general(
                 map_rows[rows, :].astype(jnp.bfloat16),
                 state[request],
@@ -360,25 +374,15 @@
             )
             for block in range(4):
                 carried[block, rows, :] = product[:, block * 128 : (block + 1) * 128]
-        return carry
-
-    lax.fori_loop(0, 2, carry_over, 0)
-    for name in ("value_cache", "value_kernel", "value_offset", "out_gain"):
-        loads[name].wait()
-
-    offset_row = value_offset[...].astype(jnp.float32).reshape(1, 512)
-    for block in range(4):
-        columns = slice(block * 128, (block + 1) * 128)
-        lane = lax.broadcasted_iota(jnp.int32, (8, 128), 1)
-        skip = jnp.where(
-            lane < 64,
-            jnp.broadcast_to(skip_gain[:, 2 * block : 2 * block + 1], (8, 128)),
-            jnp.broadcast_to(skip_gain[:, 2 * block + 1 : 2 * block + 2], (8, 128)),
-        )
-        taps = [value_kernel[k : k + 1, columns].astype(jnp.float32) for k in range(4)]
-        offset = offset_row[:, columns]
-        for tile in range(3):
-            eight = pl.ds(tile * 8, 8)
+        for block in range(4):
+            columns = slice(block * 128, (block + 1) * 128)
+            skip = jnp.where(
+                lane < 64,
+                jnp.broadcast_to(skip_gain[:, 2 * block : 2 * block + 1], (8, 128)),
+                jnp.broadcast_to(skip_gain[:, 2 * block + 1 : 2 * block + 2], (8, 128)),
+            )
+            taps = [value_kernel[k : k + 1, columns].astype(jnp.float32) for k in range(4)]
+            offset = offset_row[:, columns]
             counts = kept[tile * 8 : tile * 8 + 8]
             sequence = [value_cache[t, eight, columns].astype(jnp.float32) for t in range(3)] + [
                 rounded(inner[4 + block, pl.ds(tile * 64 + s, 8, stride=8), :])
@@ -412,57 +416,51 @@
                 gated_rows[block, pl.ds(tile * 64 + s, 8, stride=8), :] = jnp.where(
                     valid, gated * out_gain[:, columns], 0.0
                 )
-    lanes = lax.broadcasted_iota(jnp.int32, (24, 128), 1)
-    own = jnp.zeros((24, 128), jnp.float32)
-    for s in range(8):
-        own = jnp.where(lanes == s, jnp.sum(squares[s], axis=1, keepdims=True), own)
-    square_own[...] = own
-    square_swap = pltpu.make_async_remote_copy(
-        src_ref=square_own,
-        dst_ref=square_other,
-        send_sem=swap_sems.at[2],
-        recv_sem=swap_sems.at[3],
-        device_id=mate,
-        device_id_type=MESH,
-    )
-    square_swap.start()
-    for block in range(4):
-        rows_ref[:, block * 128 : (block + 1) * 128] = gated_rows[block].astype(jnp.bfloat16)
+            rows_ref[tile * 64 : tile * 64 + 64, columns] = gated_rows[
+                block, tile * 64 : tile * 64 + 64, :
+            ].astype(jnp.bfloat16)
+        own = jnp.zeros((8, 128), jnp.float32)
+        for s in range(8):
+            own = jnp.where(lane == s, jnp.sum(squares[s, eight], axis=1, keepdims=True), own)
+        square_own[tile] = own
+        copy = remote(
+            square_own.at[tile],
+            square_other.at[tile],
+            swap_sems.at[2 + tile],
+            swap_sems.at[5 + tile],
+            mate,
+        )
+        copy.start()
+        square_copies.append(copy)
     loads["out_weight"].wait()
     firsts = [along_y, along_z]
     seconds = [along_z, along_y]
     first_at = [y, z]
     second_at = [z, y]
-    copies = []
 
     def launch(src, dst, stage, route, chunk, slot, place):
-        copy = remote(src, dst, (send_sems, recv_sems, (stage, route, chunk, slot)), place)
+        copy = remote(src, dst, send_sems.at[0], recv_sems.at[stage, route, chunk, slot], place)
         copy.start()
-        copies.append(copy)
         return copy
 
     def product_of(route, step, chunk):
-        base = ((first_at[route] + step) % 4) * 1024 + chunk * 512
+        base = ((first_at[route] + step) % 4) * 1024
         return jnp.dot(
-            rows_ref[pl.ds(route * 96, 96), :],
-            out_weight[:, pl.ds(pl.multiple_of(base, 512), 512)],
+            rows_ref[pl.ds(chunk * 64 + route * 32, 32), :],
+            out_weight[:, pl.ds(pl.multiple_of(base, 1024), 1024)],
             preferred_element_type=jnp.float32,
         )
 
     def settle(route, step, chunk, product):
-        scale = scale_rows[pl.ds(route * 96, 96), :]
+        scale = scale_rows[pl.ds(chunk * 64 + route * 32, 32), :]
         partial[route, step, chunk] = (
-            product * jnp.concatenate([scale] * 4, axis=1)
+            product * jnp.concatenate([scale] * 8, axis=1)
         ).astype(jnp.bfloat16)
 
     for step in (2, 1, 3):
         for route in range(2):
             first_products[route, step - 1] = product_of(route, step, 0)
     turned[...] = jnp.transpose(weighted[...]).astype(jnp.bfloat16)
-    square_swap.wait_recv()
-    scales = lax.rsqrt((square_own[...] + square_other[...]) / 1024.0 + EPSILON)
-    for s in range(8):
-        scale_rows[pl.ds(s, 24, stride=8), :] = jnp.broadcast_to(scales[:, s : s + 1], (24, 128))
 
     def keep_states(first, last):
         owner = lax.rem(lax.broadcasted_iota(jnp.int32, (192, 128), 0), 24)
@@ -492,35 +490,40 @@
         lax.fori_loop(first, last, keep, 0)
 
     held = {}
-    for chunk in range(2):
+    for chunk in range(3):
+        square_copies[chunk].wait_recv()
+        scales = lax.rsqrt((square_own[chunk] + square_other[chunk]) / 1024.0 + EPSILON)
+        for s in range(8):
+            scale_rows[pl.ds(chunk * 64 + s, 8, stride=8), :] = jnp.broadcast_to(
+                scales[:, s : s + 1], (8, 128)
+            )
         for step in (2, 1, 3):
             for route in range(2):
-                product = first_products[route, step - 1] if chunk == 0 else product_of(route, step, 1)
+                product = first_products[route, step - 1] if chunk == 0 else product_of(route, step, chunk)
                 settle(route, step, chunk, product)
                 unit = partial.at[route, step, chunk]
                 landing = first_recv.at[route, chunk]
                 plus, minus = (firsts[route][1], firsts[route][3])
                 sends = {
-                    2: ((TOP, 0, plus), (BOTTOM, 1, minus)),
-                    1: ((BOTTOM, 3, plus),),
-                    3: ((TOP, 4, minus),),
+                    2: ((0, 0, plus), (1, 1, minus)),
+                    1: ((1, 3, plus),),
+                    3: ((0, 4, minus),),
                 }[step]
-                for rows, slot, place in sends:
+                for half, slot, place in sends:
                     held[route, chunk, slot] = launch(
-                        unit.at[rows], landing.at[slot], 0, route, chunk, slot, place
+                        unit.at[:, HALVES[half]], landing.at[slot], 0, route, chunk, slot, place
                     )
-    for chunk in range(2):
+    for chunk in range(3):
         for route in range(2):
             settle(route, 0, chunk, product_of(route, 0, chunk))
-    for chunk in range(2):
+    for chunk in range(3):
         for half in range(2):
             for route in range(2):
-                rows = (TOP, BOTTOM)[half]
                 landing = first_recv.at[route, chunk]
                 held[route, chunk, half].wait_recv()
                 mix = first_mix.at[route, chunk, half]
                 mix[...] = widened_sum(
-                    landing.at[half], partial.at[route, (1, 3)[half], chunk, rows]
+                    landing.at[half], partial.at[route, (1, 3)[half], chunk, :, HALVES[half]]
                 )
                 slot = (2, 5)[half]
                 held[route, chunk, slot] = launch(
@@ -554,53 +557,60 @@
                 started[route][index].wait_recv()
 
     def middle(route, chunk, half, k):
-        return gathered.at[route, chunk, (second_at[route] + k) % 4, (TOP, BOTTOM)[half]]
+        return gathered.at[route, chunk, (second_at[route] + k) % 4, :, HALVES[half]]
 
     def spot(route, chunk, half, k):
-        column = ((first_at[route] + k) % 4) * 1024 + chunk * 512
+        column = ((first_at[route] + k) % 4) * 1024 + half * 512
         return out_ref.at[
-            pl.ds(route * 96 + half * 48, 48), pl.ds(pl.multiple_of(column, 512), 512)
+            pl.ds(chunk * 64 + route * 32, 32), pl.ds(pl.multiple_of(column, 512), 512)
         ]
 
     inner_spread = []
-    for chunk in range(2):
+    for chunk in range(3):
         for half in range(2):
             for route in range(2):
-                rows = (TOP, BOTTOM)[half]
                 for slot in ((4, 2), (3, 5))[half]:
                     held[route, chunk, slot].wait_recv()
                 own = middle(route, chunk, half, 0)
                 own[...] = widened_sum(
-                    partial.at[route, 0, chunk, rows],
+                    partial.at[route, 0, chunk, :, HALVES[half]],
                     first_recv.at[route, chunk, 2 + half],
                     first_recv.at[route, chunk, 4 + half],
                 )
         inner_spread.append(spread_start(1, seconds, middle, chunk))
-    keep_states(0, 6)
-    for chunk in range(2):
+    pltpu.make_async_copy(
+        count_buf.at[pl.ds(1, 7)], count_buf.at[pl.ds(1, 7)], count_sems.at[1]
+    ).wait()
+    everyone = count_buf[0]
+    for d in range(1, 8):
+        everyone = everyone + count_buf[d]
+    total_own[0] = jnp.sum(everyone[0:1, 0:1]).astype(jnp.int32)
+    total_copy = pltpu.make_async_copy(total_own, total_ref, swap_sems.at[8])
+    total_copy.start()
+    keep_states(0, 4)
+    for chunk in range(3):
         spread_forward(inner_spread[chunk], 1, seconds, middle, chunk)
     outer_spread = []
-    for chunk in range(2):
+    for chunk in range(3):
         spread_finish(inner_spread[chunk])
         for half in range(2):
             for route in range(2):
-                rows = (TOP, BOTTOM)[half]
                 own = spot(route, chunk, half, 0)
-                own[...] = widened_sum(*(gathered.at[route, chunk, b, rows] for b in range(4)))
+                own[...] = widened_sum(*(gathered.at[route, chunk, b, :, HALVES[half]] for b in range(4)))
         outer_spread.append(spread_start(2, firsts, spot, chunk))
-    keep_states(6, 12)
-    for chunk in range(2):
+    for chunk in range(3):
         spread_forward(outer_spread[chunk], 2, firsts, spot, chunk)
-    for chunk in range(2):
+    keep_states(4, 12)
+    for chunk in range(3):
         spread_finish(outer_spread[chunk])
-    for copy in count_copies:
-        copy.wait_recv()
-    everyone = count_buf[0]
-    for d in range(1, 8):
-        everyone = everyone + count_buf[d]
-    total_ref[0] = jnp.sum(everyone[0:1, 0:1]).astype(jnp.int32)
-    for copy in copies + count_copies + [swap, square_swap]:
+    total_copy.wait()
+    pltpu.make_async_copy(
+        count_buf.at[pl.ds(1, 7)], count_buf.at[pl.ds(1, 7)], count_sems.at[0]
+    ).wait()
+    for copy in square_copies + [swap]:
         copy.wait_send()
+    sent = in_weight.at[pl.ds(0, 13824)]
+    pltpu.make_async_copy(sent, sent, send_sems.at[0]).wait()
 
 
 def layer(*operands):
@@ -615,7 +625,7 @@
         ),
         in_specs=[pl.BlockSpec(memory_space=pltpu.HBM)] * 20,
         out_specs=(pl.BlockSpec(memory_space=pltpu.VMEM),) * 4
-        + (pl.BlockSpec(memory_space=pltpu.SMEM),),
+        + (pl.BlockSpec(memory_space=pltpu.HBM),),
         scratch_shapes=[
             pltpu.VMEM((192, 4096), jnp.bfloat16),
             pltpu.VMEM((1, 4096), jnp.float32),
@@ -655,20 +665,20 @@
             pltpu.VMEM((4, 192, 128), jnp.float32),
             pltpu.VMEM((192, 512), jnp.bfloat16),
             pltpu.VMEM((8, 24, 128), jnp.float32),
-            pltpu.VMEM((24, 128), jnp.float32),
-            pltpu.VMEM((24, 128), jnp.float32),
+            pltpu.VMEM((3, 8, 128), jnp.float32),
+            pltpu.VMEM((3, 8, 128), jnp.float32),
             pltpu.VMEM((192, 128), jnp.float32),
-            pltpu.VMEM((2, 3, 96, 512), jnp.float32),
-            pltpu.VMEM((2, 4, 2, 96, 512), jnp.bfloat16),
-            pltpu.VMEM((2, 2, 6, 48, 512), jnp.bfloat16),
-            pltpu.VMEM((2, 2, 2, 48, 512), jnp.bfloat16),
-            pltpu.VMEM((2, 2, 4, 96, 512), jnp.bfloat16),
+            pltpu.VMEM((2, 3, 32, 1024), jnp.float32),
+            pltpu.VMEM((2, 4, 3, 32, 1024), jnp.bfloat16),
+            pltpu.VMEM((2, 3, 6, 32, 512), jnp.bfloat16),
+            pltpu.VMEM((2, 3, 2, 32, 512), jnp.bfloat16),
+            pltpu.VMEM((2, 3, 4, 32, 1024), jnp.bfloat16),
             pltpu.VMEM((8, 8, 128), jnp.float32),
-            pltpu.SemaphoreType.DMA((3, 2, 2, 6)),
-            pltpu.SemaphoreType.DMA((3, 2, 2, 6)),
-            pltpu.SemaphoreType.DMA((8,)),
-            pltpu.SemaphoreType.DMA((8,)),
-            pltpu.SemaphoreType.DMA((4,)),
+            pltpu.SMEM((1,), jnp.int32),
+            pltpu.SemaphoreType.DMA((1,)),
+            pltpu.SemaphoreType.DMA((3, 2, 3, 6)),
+            pltpu.SemaphoreType.DMA((2,)),
+            pltpu.SemaphoreType.DMA((9,)),
             pltpu.SemaphoreType.DMA((20,)),
             pltpu.SemaphoreType.DMA((4,)),
             pltpu.SemaphoreType.DMA((4,)),

time: 51.1 us -> 48.1 us (0.941)
  Pallas kernels: 48.6 us -> 45.5 us
    pallas_call x1, Pallas kernels: 46.4 us -> 43.3 us  [layer(): pl.pallas_call(layer_kernel, out_shape=(jax.ShapeDtypeStruct((192, 4096),...]
where the time goes in v4:
time: 48.1 us; the launch traced here: 47.9 us
  Pallas kernels  45.5 us (95%)
  between operations  2.41 us (5%)
    pallas_call x1, Pallas kernels, layer(): pl.pallas_call(layer_kernel, out_shape=(jax.ShapeDtypeStruct((192, 4096),...  43.3 us
    pallas_call x1, Pallas kernels, place(): pl.pallas_call(place_kernel, out_shape=tuple((jax.ShapeDtypeStruct(a.shap...  2.23 us

profile of v4, /device:TPU:0, one launch (start us, length us, event | category | flops | bytes accessed | tf_op | source)
XLA Modules:
  0.0 47.9 jit_solution(16899292926932057237)
XLA Ops:
  0.6 43.3 %shard_map.227 = (bf16[192,4096]{1,0:T(8,128)(2,1)S(1)}, bf16[24,512,128]{2,1,0:T(8,128)(2,1)S(1)}, bf16[3,24,512]{2,1,0:T(8,128)(2,1)S(1)}, bf16[3,24,128]{2,1,0:T(8,128)(2,1)S(1)}, s32[1]{0:T(128)}) custom-call(bf16[192,4096]{1,0:T(8,128)(2,1)} %bitcast.24, f32[1,4096]{1,0:T(1,128)} %bitcast.28, bf16[32768,128]{1,0:T(8,128)(2,1)} %bitcast.22, ...), custom_call_target="tpu_custom_call" | custom-call | tf_op jit(solution)/shard_map/pallas_call | solution.py:617
  43.9 2.2 %shard_map.228 = (bf16[192,4096]{1,0:T(8,128)(2,1)}, bf16[24,512,128]{2,1,0:T(8,128)(2,1)}, bf16[3,24,512]{2,1,0:T(8,128)(2,1)}, bf16[3,24,128]{2,1,0:T(8,128)(2,1)}) custom-call(bf16[192,4096]{1,0:T(8,128)(2,1)S(1)} %get-tuple-element.14.refs_0_, bf16[24,512,128]{2,1,0:T(8,128)(2,1)S(1)} %get-tuple-element.15.refs_1_, ...), custom_call_target="tpu_custom_call" | custom-call | tf_op jit(solution)/shard_map/pallas_call | solution.py:705

commit v5 on v4

--- a/solution.py
+++ b/solution.py
@@ -114,7 +114,7 @@
     square_own,
     square_other,
     scale_rows,
-    first_products,
+    products,
     partial,
     first_recv,
     first_mix,
@@ -166,6 +166,9 @@
         rows = pl.ds(index * 8192, 8192)
         pltpu.make_async_copy(in_weight_in.at[rows], in_weight.at[rows], chunk_sems.at[index]).start()
 
+    load_chunk(0)
+    load_chunk(1)
+
     def column(ref):
         square = lax.broadcasted_iota(jnp.int32, (24, 24), 0) == lax.broadcasted_iota(
             jnp.int32, (24, 24), 1
@@ -173,12 +176,6 @@
         values = jnp.broadcast_to(ref[...].astype(jnp.float32), (24, 24))
         return jnp.sum(jnp.where(square, values, 0.0), axis=1, keepdims=True)
 
-    loads["step_weight"].wait()
-    for block in range(32):
-        rows = slice(block * 128, (block + 1) * 128)
-        group_weight[rows, 128:136] = jnp.transpose(
-            step_weight[:, rows].astype(jnp.float32)
-        ).astype(jnp.bfloat16)
     loads["gain"].wait()
 
     def normalize(block):
@@ -196,17 +193,16 @@
 
     for index in range(4):
         token_copies[index].wait()
-        if index in (1, 3):
-            load_chunk(index - 1)
-            load_chunk(index)
+        if index in (0, 2):
+            load_chunk(2 + index // 2)
         for block in range(3):
             normalize(index * 3 + block)
-    load("value_cache", value_cache_in, value_cache, 15)
-    load("value_kernel", value_kernel_in, value_kernel, 5)
-    load("value_offset", value_offset_in, value_offset, 6)
-    load("out_gain", out_gain_in, out_gain, 12)
-    load("state", state_in, state, 14)
-    load("out_weight", out_weight_in, out_weight, 13)
+    loads["step_weight"].wait()
+    for block in range(32):
+        rows = slice(block * 128, (block + 1) * 128)
+        group_weight[rows, 128:136] = jnp.transpose(
+            step_weight[:, rows].astype(jnp.float32)
+        ).astype(jnp.bfloat16)
     loads["group_weight"].wait()
     product = jnp.dot(normed[...], group_weight[...], preferred_element_type=jnp.float32)
     group_rows[...] = product[:, 0:128]
@@ -271,10 +267,14 @@
 
     inner[...] = jnp.zeros_like(inner)
 
+    lower = lax.broadcasted_iota(jnp.int32, (256, 8, 128), 1) < 4
+
     def widen(start, spread):
-        spread[...] = in_weight[pl.ds(pl.multiple_of(start * 4096, 4096), 4096), :].astype(
-            jnp.float32
-        )
+        block = in_weight[pl.ds(pl.multiple_of(start * 4096, 4096), 4096), :].astype(jnp.float32)
+        block = block.reshape(256, 16, 128)
+        even, odd = block[:, 0:8], block[:, 8:16]
+        spread[0] = jnp.where(lower, even, pltpu.roll(odd, 4, 1)).reshape(2048, 128)
+        spread[1] = jnp.where(lower, pltpu.roll(even, 4, 1), odd).reshape(2048, 128)
 
     def multiply(start, spread):
         left = normed[:, pl.ds(pl.multiple_of(start * 512, 512), 512)]
@@ -282,7 +282,7 @@
             for j in range(0, 4, 2):
                 right = jnp.concatenate(
                     [
-                        spread[pl.ds((j + i) * 2 + part, 512, stride=8), :].astype(jnp.bfloat16)
+                        spread[j // 2, pl.ds(i * 2 + part, 512, stride=4), :].astype(jnp.bfloat16)
                         for i in range(2)
                     ],
                     axis=1,
@@ -307,7 +307,15 @@
 
     await_chunk(0)
     widen(0, spread_a)
-    lax.fori_loop(0, 3, pair, 0)
+    lax.fori_loop(0, 2, pair, 0)
+    load("value_cache", value_cache_in, value_cache, 15)
+    load("value_kernel", value_kernel_in, value_kernel, 5)
+    load("value_offset", value_offset_in, value_offset, 6)
+    load("out_gain", out_gain_in, out_gain, 12)
+    load("state", state_in, state, 14)
+    load("out_weight", out_weight_in, out_weight, 13)
+    lax.fori_loop(2, 3, pair, 0)
+    swap.wait_recv()
     multiply(6, spread_a)
     widen(7, spread_b)
     multiply(7, spread_b)
@@ -332,7 +340,6 @@
     head_decay = jnp.exp(prefix_kept)
     for h in range(8):
         decay_kept[h] = jnp.broadcast_to(head_decay[:, h : h + 1], (24, 128))
-    swap.wait_recv()
     for s in range(8):
         map_rows[pl.ds(s, 24, stride=8), :] = maps[1, s]
         input_rows[pl.ds(s * 24, 24), :] = maps[0, s]
@@ -416,9 +423,10 @@
                 gated_rows[block, pl.ds(tile * 64 + s, 8, stride=8), :] = jnp.where(
                     valid, gated * out_gain[:, columns], 0.0
                 )
-            rows_ref[tile * 64 : tile * 64 + 64, columns] = gated_rows[
-                block, tile * 64 : tile * 64 + 64, :
-            ].astype(jnp.bfloat16)
+            for route in range(2):
+                rows_ref[route * 96 + tile * 32 : route * 96 + tile * 32 + 32, columns] = gated_rows[
+                    block, tile * 64 + route * 32 : tile * 64 + route * 32 + 32, :
+                ].astype(jnp.bfloat16)
         own = jnp.zeros((8, 128), jnp.float32)
         for s in range(8):
             own = jnp.where(lane == s, jnp.sum(squares[s, eight], axis=1, keepdims=True), own)
@@ -438,28 +446,41 @@
     first_at = [y, z]
     second_at = [z, y]
 
+    def sem_at(stage, chunk):
+        return chunk * 18 + (0, 8, 13)[stage]
+
     def launch(src, dst, stage, route, chunk, slot, place):
-        copy = remote(src, dst, send_sems.at[0], recv_sems.at[stage, route, chunk, slot], place)
+        if slot < 2:
+            index = route * 2 + slot
+        elif stage:
+            index = 4
+        else:
+            index = 4 + route * 2 + (slot - 2) // 2
+        landed = recv_sems.at[sem_at(stage, chunk) + index]
+        copy = remote(src, dst, send_sems.at[0], landed, place)
         copy.start()
         return copy
 
-    def product_of(route, step, chunk):
+    def await_bytes(ref, stage, chunk, index):
+        pltpu.make_async_copy(ref, ref, recv_sems.at[sem_at(stage, chunk) + index]).wait()
+
+    def multiply_out(route, step):
         base = ((first_at[route] + step) % 4) * 1024
-        return jnp.dot(
-            rows_ref[pl.ds(chunk * 64 + route * 32, 32), :],
+        products[route, step] = jnp.dot(
+            rows_ref[pl.ds(route * 96, 96), :],
             out_weight[:, pl.ds(pl.multiple_of(base, 1024), 1024)],
             preferred_element_type=jnp.float32,
         )
 
-    def settle(route, step, chunk, product):
+    def settle(route, step, chunk):
         scale = scale_rows[pl.ds(chunk * 64 + route * 32, 32), :]
         partial[route, step, chunk] = (
-            product * jnp.concatenate([scale] * 8, axis=1)
+            products[route, step, pl.ds(chunk * 32, 32), :] * jnp.concatenate([scale] * 8, axis=1)
         ).astype(jnp.bfloat16)
 
-    for step in (2, 1, 3):
+    for step in (2, 1, 3, 0):
         for route in range(2):
-            first_products[route, step - 1] = product_of(route, step, 0)
+            multiply_out(route, step)
     turned[...] = jnp.transpose(weighted[...]).astype(jnp.bfloat16)
 
     def keep_states(first, last):
@@ -497,25 +518,35 @@
             scale_rows[pl.ds(chunk * 64 + s, 8, stride=8), :] = jnp.broadcast_to(
                 scales[:, s : s + 1], (8, 128)
             )
-        for step in (2, 1, 3):
-            for route in range(2):
-                product = first_products[route, step - 1] if chunk == 0 else product_of(route, step, chunk)
-                settle(route, step, chunk, product)
-                unit = partial.at[route, step, chunk]
-                landing = first_recv.at[route, chunk]
-                plus, minus = (firsts[route][1], firsts[route][3])
-                sends = {
-                    2: ((0, 0, plus), (1, 1, minus)),
-                    1: ((1, 3, plus),),
-                    3: ((0, 4, minus),),
-                }[step]
-                for half, slot, place in sends:
-                    held[route, chunk, slot] = launch(
-                        unit.at[:, HALVES[half]], landing.at[slot], 0, route, chunk, slot, place
-                    )
-    for chunk in range(3):
         for route in range(2):
-            settle(route, 0, chunk, product_of(route, 0, chunk))
+            settle(route, 2, chunk)
+            for half in range(2):
+                held[route, chunk, half] = launch(
+                    partial.at[route, 2, chunk, :, HALVES[half]],
+                    first_recv.at[route, chunk, half],
+                    0,
+                    route,
+                    chunk,
+                    half,
+                    firsts[route][(1, 3)[half]],
+                )
+    for chunk in range(3):
+        for route in range(2):
+            for step, half, slot in ((1, 1, 4), (3, 0, 3)):
+                settle(route, step, chunk)
+                launch(
+                    partial.at[route, step, chunk, :, HALVES[half]],
+                    first_recv.at[route, chunk, slot],
+                    0,
+                    route,
+                    chunk,
+                    slot,
+                    firsts[route][step],
+                )
+    for chunk in range(3):
+        for route in range(2):
+            settle(route, 0, chunk)
+    keep_states(0, 7)
     for chunk in range(3):
         for half in range(2):
             for route in range(2):
@@ -530,13 +561,14 @@
                     mix, landing.at[slot], 0, route, chunk, slot, firsts[route][(1, 3)[half]]
                 )
 
-    def spread_start(stage, places, piece, chunk):
+    def spread_start(stage, places, piece, chunk, crossed):
         started = []
         for route in range(2):
-            plus, minus = (places[route][1], places[route][3])
             started.append([])
-            for half, slot, place in ((0, 0, plus), (1, 1, minus), (1, 2, plus), (0, 3, minus)):
+            for half in range(2):
                 own = piece(route, chunk, half, 0)
+                place = places[route][(1, 3)[half ^ crossed]]
+                slot = 2 * crossed + half
                 started[route].append(launch(own, own, stage, route, chunk, slot, place))
         return started
 
@@ -545,16 +577,10 @@
             for route in range(2):
                 started[route][half].wait_recv()
                 passed = piece(route, chunk, half, (3, 1)[half])
-                started[route].append(
-                    launch(
-                        passed, passed, stage, route, chunk, 4 + half, places[route][(1, 3)[half]]
-                    )
-                )
-
-    def spread_finish(started):
-        for route in range(2):
-            for index in range(2, 6):
-                started[route][index].wait_recv()
+                launch(passed, passed, stage, route, chunk, 4 + half, places[route][(1, 3)[half]])
+
+    def spread_finish(stage, chunk):
+        await_bytes(in_weight.at[pl.ds(0, 1024)], stage, chunk, 4)
 
     def middle(route, chunk, half, k):
         return gathered.at[route, chunk, (second_at[route] + k) % 4, :, HALVES[half]]
@@ -569,15 +595,17 @@
     for chunk in range(3):
         for half in range(2):
             for route in range(2):
-                for slot in ((4, 2), (3, 5))[half]:
-                    held[route, chunk, slot].wait_recv()
+                pair_ref = first_recv.at[route, chunk, pl.ds(2 + 2 * half, 2)]
+                await_bytes(pair_ref, 0, chunk, 4 + route * 2 + half)
                 own = middle(route, chunk, half, 0)
                 own[...] = widened_sum(
                     partial.at[route, 0, chunk, :, HALVES[half]],
-                    first_recv.at[route, chunk, 2 + half],
-                    first_recv.at[route, chunk, 4 + half],
-                )
-        inner_spread.append(spread_start(1, seconds, middle, chunk))
+                    first_recv.at[route, chunk, 2 + 2 * half],
+                    first_recv.at[route, chunk, 3 + 2 * half],
+                )
+        inner_spread.append(spread_start(1, seconds, middle, chunk, 0))
+    for chunk in range(3):
+        spread_start(1, seconds, middle, chunk, 1)
     pltpu.make_async_copy(
         count_buf.at[pl.ds(1, 7)], count_buf.at[pl.ds(1, 7)], count_sems.at[1]
     ).wait()
@@ -587,22 +615,23 @@
     total_own[0] = jnp.sum(everyone[0:1, 0:1]).astype(jnp.int32)
     total_copy = pltpu.make_async_copy(total_own, total_ref, swap_sems.at[8])
     total_copy.start()
-    keep_states(0, 4)
     for chunk in range(3):
         spread_forward(inner_spread[chunk], 1, seconds, middle, chunk)
     outer_spread = []
     for chunk in range(3):
-        spread_finish(inner_spread[chunk])
+        spread_finish(1, chunk)
         for half in range(2):
             for route in range(2):
                 own = spot(route, chunk, half, 0)
                 own[...] = widened_sum(*(gathered.at[route, chunk, b, :, HALVES[half]] for b in range(4)))
-        outer_spread.append(spread_start(2, firsts, spot, chunk))
+        outer_spread.append(spread_start(2, firsts, spot, chunk, 0))
+    for chunk in range(3):
+        spread_start(2, firsts, spot, chunk, 1)
     for chunk in range(3):
         spread_forward(outer_spread[chunk], 2, firsts, spot, chunk)
-    keep_states(4, 12)
-    for chunk in range(3):
-        spread_finish(outer_spread[chunk])
+    keep_states(7, 12)
+    for chunk in range(3):
+        spread_finish(2, chunk)
     total_copy.wait()
     pltpu.make_async_copy(
         count_buf.at[pl.ds(1, 7)], count_buf.at[pl.ds(1, 7)], count_sems.at[0]
@@ -648,8 +677,8 @@
             pltpu.VMEM((1, 24), jnp.int32),
             pltpu.VMEM((1, 24), jnp.int32),
             pltpu.VMEM((192, 4096), jnp.bfloat16),
-            pltpu.VMEM((4096, 128), jnp.float32),
-            pltpu.VMEM((4096, 128), jnp.float32),
+            pltpu.VMEM((2, 2048, 128), jnp.float32),
+            pltpu.VMEM((2, 2048, 128), jnp.float32),
             pltpu.VMEM((8, 192, 128), jnp.float32),
             pltpu.VMEM((192, 128), jnp.float32),
             pltpu.VMEM((192, 128), jnp.float32),
@@ -668,7 +697,7 @@
             pltpu.VMEM((3, 8, 128), jnp.float32),
             pltpu.VMEM((3, 8, 128), jnp.float32),
             pltpu.VMEM((192, 128), jnp.float32),
-            pltpu.VMEM((2, 3, 32, 1024), jnp.float32),
+            pltpu.VMEM((2, 4, 96, 1024), jnp.float32),
             pltpu.VMEM((2, 4, 3, 32, 1024), jnp.bfloat16),
             pltpu.VMEM((2, 3, 6, 32, 512), jnp.bfloat16),
             pltpu.VMEM((2, 3, 2, 32, 512), jnp.bfloat16),
@@ -676,7 +705,7 @@
             pltpu.VMEM((8, 8, 128), jnp.float32),
             pltpu.SMEM((1,), jnp.int32),
             pltpu.SemaphoreType.DMA((1,)),
-            pltpu.SemaphoreType.DMA((3, 2, 3, 6)),
+            pltpu.SemaphoreType.DMA((54,)),
             pltpu.SemaphoreType.DMA((2,)),
             pltpu.SemaphoreType.DMA((9,)),
             pltpu.SemaphoreType.DMA((20,)),
@@ -690,14 +719,20 @@
 
 
 def place_kernel(*refs):
-    sources, targets, sems = refs[:4], refs[4:8], refs[8]
+    sources, total, targets, total_out = refs[:4], refs[4], refs[5:9], refs[9]
+    held, sems = refs[10:]
+    inward = pltpu.make_async_copy(total, held, sems.at[4])
+    inward.start()
     copies = [
         pltpu.make_async_copy(source, target, sems.at[index])
         for index, (source, target) in enumerate(zip(sources, targets))
     ]
     for copy in copies:
         copy.start()
-    for copy in copies:
+    inward.wait()
+    outward = pltpu.make_async_copy(held, total_out, sems.at[5])
+    outward.start()
+    for copy in copies + [outward]:
         copy.wait()
 
 
@@ -705,9 +740,10 @@
     return pl.pallas_call(
         place_kernel,
         out_shape=tuple(jax.ShapeDtypeStruct(a.shape, a.dtype) for a in arrays),
-        in_specs=[pl.BlockSpec(memory_space=pltpu.VMEM)] * 4,
-        out_specs=(pl.BlockSpec(memory_space=pltpu.HBM),) * 4,
-        scratch_shapes=[pltpu.SemaphoreType.DMA((4,))],
+        in_specs=[pl.BlockSpec(memory_space=pltpu.VMEM)] * 4
+        + [pl.BlockSpec(memory_space=pltpu.HBM)],
+        out_specs=(pl.BlockSpec(memory_space=pltpu.HBM),) * 5,
+        scratch_shapes=[pltpu.SMEM((1,), jnp.int32), pltpu.SemaphoreType.DMA((6,))],
         compiler_params=pltpu.CompilerParams(vmem_limit_bytes=16 * 1024 * 1024),
     )(*arrays)
 
@@ -757,7 +793,9 @@
         draft_lengths.reshape(1, 24),
         live_flags.reshape(1, 24),
     )
-    rows, kept_state, value_kept, group_kept = place(rows, kept_state, value_kept, group_kept)
+    rows, kept_state, value_kept, group_kept, total = place(
+        rows, kept_state, value_kept, group_kept, total
+    )
     return (
         rows.reshape(24, 8, 4096),
         kept_state.reshape(24, 8, 64, 128),

time: 48.1 us -> 44.2 us (0.919)
  Pallas kernels: 45.5 us -> 43.4 us
  between operations: 2.41 us -> 0.65 us
    pallas_call x1, Pallas kernels: 43.3 us -> 40.5 us  [layer(): pl.pallas_call(layer_kernel, out_shape=(jax.ShapeDtypeStruct((192, 4096),...]
    pallas_call x1, Pallas kernels: 2.23 us -> 2.88 us  [place(): pl.pallas_call(place_kernel, out_shape=tuple((jax.ShapeDtypeStruct(a.shap...]
where the time goes in v5:
time: 44.2 us; the launch traced here: 44 us
  Pallas kernels  43.4 us (98%)
  between operations  0.65 us (1%)
    pallas_call x1, Pallas kernels, layer(): pl.pallas_call(layer_kernel, out_shape=(jax.ShapeDtypeStruct((192, 4096),...  40.5 us
    pallas_call x1, Pallas kernels, place(): pl.pallas_call(place_kernel, out_shape=tuple((jax.ShapeDtypeStruct(a.shap...  2.88 us

profile of v5, /device:TPU:0, one launch (start us, length us, event | category | flops | bytes accessed | tf_op | source)
XLA Modules:
  0.0 44.0 jit_solution(14780542637033347399)
XLA Ops:
  0.6 40.5 %shard_map.227 = (bf16[192,4096]{1,0:T(8,128)(2,1)S(1)}, bf16[24,512,128]{2,1,0:T(8,128)(2,1)S(1)}, bf16[3,24,512]{2,1,0:T(8,128)(2,1)S(1)}, bf16[3,24,128]{2,1,0:T(8,128)(2,1)S(1)}, s32[1]{0:T(128)}) custom-call(bf16[192,4096]{1,0:T(8,128)(2,1)} %bitcast.24, f32[1,4096]{1,0:T(1,128)} %bitcast.28, bf16[32768,128]{1,0:T(8,128)(2,1)} %bitcast.22, ...), custom_call_target="tpu_custom_call" | custom-call | tf_op jit(solution)/shard_map/pallas_call | solution.py:646
  41.1 2.9 %shard_map.228 = (bf16[192,4096]{1,0:T(8,128)(2,1)}, bf16[24,512,128]{2,1,0:T(8,128)(2,1)}, bf16[3,24,512]{2,1,0:T(8,128)(2,1)}, bf16[3,24,128]{2,1,0:T(8,128)(2,1)}, s32[1]{0:T(128)}) custom-call(bf16[192,4096]{1,0:T(8,128)(2,1)S(1)} %get-tuple-element.15.refs_0_, bf16[24,512,128]{2,1,0:T(8,128)(2,1)S(1)} %get-tuple-element.16.refs_1_, ...), custom_call_target="tpu_custom_call" | custom-call | tf_op jit(solution)/shard_map/pallas_call | solution.py:740

commit v6 on v5

--- a/solution.py
+++ b/solution.py
@@ -120,7 +120,6 @@
     first_mix,
     gathered,
     count_buf,
-    total_own,
     send_sems,
     recv_sems,
     count_sems,
@@ -136,8 +135,6 @@
     barrier = pltpu.get_barrier_semaphore()
     dp_peers = [{"dp": (dp + d) % 8} for d in range(1, 8)]
     ring_peers = [along_z[1], along_z[3], along_y[1], along_y[3]]
-    for place in ring_peers + dp_peers:
-        pl.semaphore_signal(barrier, inc=1, device_id=place, device_id_type=MESH)
     loads = {}
 
     def load(name, src, dst, index):
@@ -151,6 +148,8 @@
         copy.start()
         token_copies.append(copy)
     load("gain", gain_in, gain, 1)
+    for place in ring_peers + dp_peers:
+        pl.semaphore_signal(barrier, inc=1, device_id=place, device_id_type=MESH)
     load("step_weight", step_weight_in, step_weight, 4)
     load("group_weight", group_weight_in, group_weight.at[:, 0:128], 3)
     load("accepted", accepted_in, accepted, 17)
@@ -315,7 +314,6 @@
     load("state", state_in, state, 14)
     load("out_weight", out_weight_in, out_weight, 13)
     lax.fori_loop(2, 3, pair, 0)
-    swap.wait_recv()
     multiply(6, spread_a)
     widen(7, spread_b)
     multiply(7, spread_b)
@@ -330,23 +328,29 @@
         steps.append(size)
         after.append(running)
     prefix_kept = jnp.zeros_like(running)
+
+    def keep_small(q, value):
+        for tile in range(3):
+            small[pl.ds(tile * 416 + q * 8, 8), 0:8] = value[tile * 8 : tile * 8 + 8]
+
     for s in range(8):
         prefix_kept = jnp.where(kept == float(s + 1), after[s], prefix_kept)
     for s in range(8):
-        small[pl.ds((36 + s) * 24, 24), 0:8] = jnp.exp(after[s])
-        small[pl.ds((44 + s) * 24, 24), 0:8] = (
-            jnp.where(kept > float(s), jnp.exp(prefix_kept - after[s]), 0.0) * steps[s]
+        keep_small(36 + s, jnp.exp(after[s]))
+        keep_small(
+            44 + s, jnp.where(kept > float(s), jnp.exp(prefix_kept - after[s]), 0.0) * steps[s]
         )
     head_decay = jnp.exp(prefix_kept)
     for h in range(8):
         decay_kept[h] = jnp.broadcast_to(head_decay[:, h : h + 1], (24, 128))
+    swap.wait_recv()
     for s in range(8):
         map_rows[pl.ds(s, 24, stride=8), :] = maps[1, s]
         input_rows[pl.ds(s * 24, 24), :] = maps[0, s]
         for j in range(s + 1):
             match = jnp.sum(maps[1, s] * maps[0, j], axis=1, keepdims=True)
-            small[pl.ds((s * (s + 1) // 2 + j) * 24, 24), 0:8] = (
-                jnp.exp(after[s] - after[j]) * steps[j] * match
+            keep_small(
+                s * (s + 1) // 2 + j, jnp.exp(after[s] - after[j]) * steps[j] * match
             )
     hot = (
         lax.broadcasted_iota(jnp.int32, (8, 512), 1) // 64
@@ -360,8 +364,6 @@
         )
         return carry
 
-    for index in range(3):
-        expand(index, 0)
     loads["state"].wait()
 
     for name in ("value_cache", "value_kernel", "value_offset", "out_gain"):
@@ -370,6 +372,7 @@
     lane = lax.broadcasted_iota(jnp.int32, (8, 128), 1)
     square_copies = []
     for tile in range(3):
+        expand(tile, 0)
         eight = pl.ds(tile * 8, 8)
         for request in range(tile * 8, tile * 8 + 8):
             rows = pl.ds(request * 8, 8)
@@ -400,16 +403,16 @@
             values = convolved(sequence, taps, offset)
             for s in range(8):
                 weighted[pl.ds(s * 24 + tile * 8, 8), columns] = (
-                    mixing[pl.ds((44 + s) * 24 + tile * 8, 8), columns] * values[s]
+                    mixing[pl.ds(tile * 416 + (44 + s) * 8, 8), columns] * values[s]
                 )
                 total = (
-                    mixing[pl.ds((36 + s) * 24 + tile * 8, 8), columns]
+                    mixing[pl.ds(tile * 416 + (36 + s) * 8, 8), columns]
                     * carried[block, pl.ds(tile * 64 + s, 8, stride=8), :]
                     + skip * values[s]
                 )
                 for j in range(s + 1):
                     q = s * (s + 1) // 2 + j
-                    total = total + mixing[pl.ds(q * 24 + tile * 8, 8), columns] * values[j]
+                    total = total + mixing[pl.ds(tile * 416 + q * 8, 8), columns] * values[j]
                 gate = rounded(inner[block, pl.ds(tile * 64 + s, 8, stride=8), :])
                 gated = total * (gate / (1.0 + jnp.exp(-gate)))
                 square = gated * gated
@@ -442,15 +445,18 @@
         square_copies.append(copy)
     loads["out_weight"].wait()
     firsts = [along_y, along_z]
-    seconds = [along_z, along_y]
     first_at = [y, z]
-    second_at = [z, y]
+    halving = []
+    for at, make in ((z, lambda i: i * 4 + y), (y, lambda i: z * 4 + i)):
+        halving.append([{"tensor": make(at + 1 - 2 * (at % 2))}, {"tensor": make(3 - at)}])
 
     def sem_at(stage, chunk):
-        return chunk * 18 + (0, 8, 13)[stage]
+        return chunk * 21 + (0, 8, 16)[stage]
 
     def launch(src, dst, stage, route, chunk, slot, place):
-        if slot < 2:
+        if stage == 1:
+            index = route * 4 + slot
+        elif slot < 2:
             index = route * 2 + slot
         elif stage:
             index = 4
@@ -481,8 +487,6 @@
     for step in (2, 1, 3, 0):
         for route in range(2):
             multiply_out(route, step)
-    turned[...] = jnp.transpose(weighted[...]).astype(jnp.bfloat16)
-
     def keep_states(first, last):
         owner = lax.rem(lax.broadcasted_iota(jnp.int32, (192, 128), 0), 24)
 
@@ -546,6 +550,7 @@
     for chunk in range(3):
         for route in range(2):
             settle(route, 0, chunk)
+    turned[...] = jnp.transpose(weighted[...]).astype(jnp.bfloat16)
     keep_states(0, 7)
     for chunk in range(3):
         for half in range(2):
@@ -582,48 +587,67 @@
     def spread_finish(stage, chunk):
         await_bytes(in_weight.at[pl.ds(0, 1024)], stage, chunk, 4)
 
-    def middle(route, chunk, half, k):
-        return gathered.at[route, chunk, (second_at[route] + k) % 4, :, HALVES[half]]
-
     def spot(route, chunk, half, k):
         column = ((first_at[route] + k) % 4) * 1024 + half * 512
         return out_ref.at[
             pl.ds(chunk * 64 + route * 32, 32), pl.ds(pl.multiple_of(column, 512), 512)
         ]
 
-    inner_spread = []
+    paired = {}
     for chunk in range(3):
         for half in range(2):
             for route in range(2):
                 pair_ref = first_recv.at[route, chunk, pl.ds(2 + 2 * half, 2)]
                 await_bytes(pair_ref, 0, chunk, 4 + route * 2 + half)
-                own = middle(route, chunk, half, 0)
+                own = gathered.at[route, chunk, half, 0]
                 own[...] = widened_sum(
                     partial.at[route, 0, chunk, :, HALVES[half]],
                     first_recv.at[route, chunk, 2 + 2 * half],
                     first_recv.at[route, chunk, 3 + 2 * half],
                 )
-        inner_spread.append(spread_start(1, seconds, middle, chunk, 0))
-    for chunk in range(3):
-        spread_start(1, seconds, middle, chunk, 1)
+                paired[route, chunk, half] = launch(
+                    own,
+                    gathered.at[route, chunk, half, 1],
+                    1,
+                    route,
+                    chunk,
+                    half,
+                    halving[route][half],
+                )
     pltpu.make_async_copy(
         count_buf.at[pl.ds(1, 7)], count_buf.at[pl.ds(1, 7)], count_sems.at[1]
     ).wait()
     everyone = count_buf[0]
     for d in range(1, 8):
         everyone = everyone + count_buf[d]
-    total_own[0] = jnp.sum(everyone[0:1, 0:1]).astype(jnp.int32)
-    total_copy = pltpu.make_async_copy(total_own, total_ref, swap_sems.at[8])
-    total_copy.start()
-    for chunk in range(3):
-        spread_forward(inner_spread[chunk], 1, seconds, middle, chunk)
-    outer_spread = []
-    for chunk in range(3):
-        spread_finish(1, chunk)
+    total_ref[...] = everyone
+    crossed = {}
+    for chunk in range(3):
         for half in range(2):
             for route in range(2):
+                paired[route, chunk, half].wait_recv()
+                both = gathered.at[route, chunk, half, 2]
+                both[...] = widened_sum(
+                    gathered.at[route, chunk, half, 0], gathered.at[route, chunk, half, 1]
+                )
+                crossed[route, chunk, half] = launch(
+                    both,
+                    gathered.at[route, chunk, half, 3],
+                    1,
+                    route,
+                    chunk,
+                    2 + half,
+                    halving[route][1 - half],
+                )
+    outer_spread = []
+    for chunk in range(3):
+        for half in range(2):
+            for route in range(2):
+                crossed[route, chunk, half].wait_recv()
                 own = spot(route, chunk, half, 0)
-                own[...] = widened_sum(*(gathered.at[route, chunk, b, :, HALVES[half]] for b in range(4)))
+                own[...] = widened_sum(
+                    gathered.at[route, chunk, half, 2], gathered.at[route, chunk, half, 3]
+                )
         outer_spread.append(spread_start(2, firsts, spot, chunk, 0))
     for chunk in range(3):
         spread_start(2, firsts, spot, chunk, 1)
@@ -632,13 +656,12 @@
     keep_states(7, 12)
     for chunk in range(3):
         spread_finish(2, chunk)
-    total_copy.wait()
     pltpu.make_async_copy(
         count_buf.at[pl.ds(1, 7)], count_buf.at[pl.ds(1, 7)], count_sems.at[0]
     ).wait()
     for copy in square_copies + [swap]:
         copy.wait_send()
-    sent = in_weight.at[pl.ds(0, 13824)]
+    sent = in_weight.at[pl.ds(0, 12288)]
     pltpu.make_async_copy(sent, sent, send_sems.at[0]).wait()
 
 
@@ -650,11 +673,10 @@
             jax.ShapeDtypeStruct((24, 512, 128), jnp.bfloat16),
             jax.ShapeDtypeStruct((3, 24, 512), jnp.bfloat16),
             jax.ShapeDtypeStruct((3, 24, 128), jnp.bfloat16),
-            jax.ShapeDtypeStruct((1,), jnp.int32),
+            jax.ShapeDtypeStruct((8, 128), jnp.float32),
         ),
         in_specs=[pl.BlockSpec(memory_space=pltpu.HBM)] * 20,
-        out_specs=(pl.BlockSpec(memory_space=pltpu.VMEM),) * 4
-        + (pl.BlockSpec(memory_space=pltpu.HBM),),
+        out_specs=(pl.BlockSpec(memory_space=pltpu.VMEM),) * 5,
         scratch_shapes=[
             pltpu.VMEM((192, 4096), jnp.bfloat16),
             pltpu.VMEM((1, 4096), jnp.float32),
@@ -701,11 +723,10 @@
             pltpu.VMEM((2, 4, 3, 32, 1024), jnp.bfloat16),
             pltpu.VMEM((2, 3, 6, 32, 512), jnp.bfloat16),
             pltpu.VMEM((2, 3, 2, 32, 512), jnp.bfloat16),
-            pltpu.VMEM((2, 3, 4, 32, 1024), jnp.bfloat16),
+            pltpu.VMEM((2, 3, 2, 4, 32, 512), jnp.bfloat16),
             pltpu.VMEM((8, 8, 128), jnp.float32),
-            pltpu.SMEM((1,), jnp.int32),
             pltpu.SemaphoreType.DMA((1,)),
-            pltpu.SemaphoreType.DMA((54,)),
+            pltpu.SemaphoreType.DMA((63,)),
             pltpu.SemaphoreType.DMA((2,)),
             pltpu.SemaphoreType.DMA((9,)),
             pltpu.SemaphoreType.DMA((20,)),
@@ -721,16 +742,20 @@
 def place_kernel(*refs):
     sources, total, targets, total_out = refs[:4], refs[4], refs[5:9], refs[9]
     held, sems = refs[10:]
-    inward = pltpu.make_async_copy(total, held, sems.at[4])
-    inward.start()
+    pieces = []
+    for index, cuts in enumerate((2, 4, 1, 1)):
+        length = sources[index].shape[0] // cuts
+        for cut in range(cuts):
+            span = pl.ds(cut * length, length)
+            pieces.append((sources[index].at[span], targets[index].at[span]))
     copies = [
         pltpu.make_async_copy(source, target, sems.at[index])
-        for index, (source, target) in enumerate(zip(sources, targets))
+        for index, (source, target) in enumerate(pieces)
     ]
     for copy in copies:
         copy.start()
-    inward.wait()
-    outward = pltpu.make_async_copy(held, total_out, sems.at[5])
+    held[0] = jnp.sum(total[0:1, 0:1]).astype(jnp.int32)
+    outward = pltpu.make_async_copy(held, total_out, sems.at[8])
     outward.start()
     for copy in copies + [outward]:
         copy.wait()
@@ -739,11 +764,11 @@
 def place(*arrays):
     return pl.pallas_call(
         place_kernel,
-        out_shape=tuple(jax.ShapeDtypeStruct(a.shape, a.dtype) for a in arrays),
-        in_specs=[pl.BlockSpec(memory_space=pltpu.VMEM)] * 4
-        + [pl.BlockSpec(memory_space=pltpu.HBM)],
+        out_shape=tuple(jax.ShapeDtypeStruct(a.shape, a.dtype) for a in arrays[:4])
+        + (jax.ShapeDtypeStruct((1,), jnp.int32),),
+        in_specs=[pl.BlockSpec(memory_space=pltpu.VMEM)] * 5,
         out_specs=(pl.BlockSpec(memory_space=pltpu.HBM),) * 5,
-        scratch_shapes=[pltpu.SMEM((1,), jnp.int32), pltpu.SemaphoreType.DMA((6,))],
+        scratch_shapes=[pltpu.SMEM((1,), jnp.int32), pltpu.SemaphoreType.DMA((9,))],
         compiler_params=pltpu.CompilerParams(vmem_limit_bytes=16 * 1024 * 1024),
     )(*arrays)
 

time: 44.2 us -> 42.1 us (0.952)
  Pallas kernels: 43.4 us -> 41.4 us
    pallas_call x1, Pallas kernels: 40.5 us -> 39.1 us  [layer(): pl.pallas_call(layer_kernel, out_shape=(jax.ShapeDtypeStruct((192, 4096),...]
    pallas_call x1, Pallas kernels: 2.88 us -> 2.28 us  [place(): pl.pallas_call(place_kernel, out_shape=tuple((jax.ShapeDtypeStruct(a.shap...]
where the time goes in v6:
time: 42.1 us; the launch traced here: 42 us
  Pallas kernels  41.4 us (98%)
  between operations  0.65 us (2%)
    pallas_call x1, Pallas kernels, layer(): pl.pallas_call(layer_kernel, out_shape=(jax.ShapeDtypeStruct((192, 4096),...  39.1 us
    pallas_call x1, Pallas kernels, place(): pl.pallas_call(place_kernel, out_shape=tuple((jax.ShapeDtypeStruct(a.shap...  2.28 us

profile of v6, /device:TPU:0, one launch (start us, length us, event | category | flops | bytes accessed | tf_op | source)
XLA Modules:
  0.0 42.0 jit_solution(15088002446580694347)
XLA Ops:
  0.6 39.1 %shard_map.227 = (bf16[192,4096]{1,0:T(8,128)(2,1)S(1)}, bf16[24,512,128]{2,1,0:T(8,128)(2,1)S(1)}, bf16[3,24,512]{2,1,0:T(8,128)(2,1)S(1)}, bf16[3,24,128]{2,1,0:T(8,128)(2,1)S(1)}, f32[8,128]{1,0:T(8,128)S(1)}) custom-call(bf16[192,4096]{1,0:T(8,128)(2,1)} %bitcast.24, f32[1,4096]{1,0:T(1,128)} %bitcast.28, bf16[32768,128]{1,0:T(8,128)(2,1)} %bitcast.22, ...), custom_call_target="tpu_custom_call" | custom-call | tf_op jit(solution)/shard_map/pallas_call | solution.py:669
  39.8 2.3 %shard_map.228 = (bf16[192,4096]{1,0:T(8,128)(2,1)}, bf16[24,512,128]{2,1,0:T(8,128)(2,1)}, bf16[3,24,512]{2,1,0:T(8,128)(2,1)}, bf16[3,24,128]{2,1,0:T(8,128)(2,1)}, s32[1]{0:T(128)}) custom-call(bf16[192,4096]{1,0:T(8,128)(2,1)S(1)} %get-tuple-element.15.refs_0_, bf16[24,512,128]{2,1,0:T(8,128)(2,1)S(1)} %get-tuple-element.16.refs_1_, ...), custom_call_target="tpu_custom_call" | custom-call | tf_op jit(solution)/shard_map/pallas_call | solution.py:765

commit v7 on v6

--- a/solution.py
+++ b/solution.py
@@ -470,23 +470,23 @@
     def await_bytes(ref, stage, chunk, index):
         pltpu.make_async_copy(ref, ref, recv_sems.at[sem_at(stage, chunk) + index]).wait()
 
-    def multiply_out(route, step):
-        base = ((first_at[route] + step) % 4) * 1024
-        products[route, step] = jnp.dot(
-            rows_ref[pl.ds(route * 96, 96), :],
-            out_weight[:, pl.ds(pl.multiple_of(base, 1024), 1024)],
+    def multiply_out(block):
+        products[block] = jnp.dot(
+            rows_ref[...],
+            out_weight[:, block * 1024 : (block + 1) * 1024],
             preferred_element_type=jnp.float32,
         )
 
     def settle(route, step, chunk):
         scale = scale_rows[pl.ds(chunk * 64 + route * 32, 32), :]
         partial[route, step, chunk] = (
-            products[route, step, pl.ds(chunk * 32, 32), :] * jnp.concatenate([scale] * 8, axis=1)
+            products[
+                (first_at[route] + step) % 4, pl.ds(route * 96 + chunk * 32, 32), :
+            ] * jnp.concatenate([scale] * 8, axis=1)
         ).astype(jnp.bfloat16)
 
-    for step in (2, 1, 3, 0):
-        for route in range(2):
-            multiply_out(route, step)
+    for block in range(4):
+        multiply_out(block)
     def keep_states(first, last):
         owner = lax.rem(lax.broadcasted_iota(jnp.int32, (192, 128), 0), 24)
 
@@ -719,7 +719,7 @@
             pltpu.VMEM((3, 8, 128), jnp.float32),
             pltpu.VMEM((3, 8, 128), jnp.float32),
             pltpu.VMEM((192, 128), jnp.float32),
-            pltpu.VMEM((2, 4, 96, 1024), jnp.float32),
+            pltpu.VMEM((4, 192, 1024), jnp.float32),
             pltpu.VMEM((2, 4, 3, 32, 1024), jnp.bfloat16),
             pltpu.VMEM((2, 3, 6, 32, 512), jnp.bfloat16),
             pltpu.VMEM((2, 3, 2, 32, 512), jnp.bfloat16),

time: 42.1 us -> 42.3 us (level)
  no operation moved by 1% of the time
where the time goes in v7:
time: 42.3 us; the launch traced here: 42.2 us
  Pallas kernels  41.6 us (98%)
  between operations  0.65 us (2%)
    pallas_call x1, Pallas kernels, layer(): pl.pallas_call(layer_kernel, out_shape=(jax.ShapeDtypeStruct((192, 4096),...  39.3 us
    pallas_call x1, Pallas kernels, place(): pl.pallas_call(place_kernel, out_shape=tuple((jax.ShapeDtypeStruct(a.shap...  2.28 us

profile of v7, /device:TPU:0, one launch (start us, length us, event | category | flops | bytes accessed | tf_op | source)
XLA Modules:
  0.0 42.2 jit_solution(11367804955594770941)
XLA Ops:
  0.6 39.3 %shard_map.227 = (bf16[192,4096]{1,0:T(8,128)(2,1)S(1)}, bf16[24,512,128]{2,1,0:T(8,128)(2,1)S(1)}, bf16[3,24,512]{2,1,0:T(8,128)(2,1)S(1)}, bf16[3,24,128]{2,1,0:T(8,128)(2,1)S(1)}, f32[8,128]{1,0:T(8,128)S(1)}) custom-call(bf16[192,4096]{1,0:T(8,128)(2,1)} %bitcast.24, f32[1,4096]{1,0:T(1,128)} %bitcast.28, bf16[32768,128]{1,0:T(8,128)(2,1)} %bitcast.22, ...), custom_call_target="tpu_custom_call" | custom-call | tf_op jit(solution)/shard_map/pallas_call | solution.py:669
  39.9 2.3 %shard_map.228 = (bf16[192,4096]{1,0:T(8,128)(2,1)}, bf16[24,512,128]{2,1,0:T(8,128)(2,1)}, bf16[3,24,512]{2,1,0:T(8,128)(2,1)}, bf16[3,24,128]{2,1,0:T(8,128)(2,1)}, s32[1]{0:T(128)}) custom-call(bf16[192,4096]{1,0:T(8,128)(2,1)S(1)} %get-tuple-element.15.refs_0_, bf16[24,512,128]{2,1,0:T(8,128)(2,1)S(1)} %get-tuple-element.16.refs_1_, ...), custom_call_target="tpu_custom_call" | custom-call | tf_op jit(solution)/shard_map/pallas_call | solution.py:765
